TPU v7x, 256 devices: a whole 4x4x8 slice. The times are simulated.
256 devices in a mesh: row: 16 (over y_lo, x, core), col: 16 (over z, y_hi).
Axes of the slice: x: 4, y: 4 (y_hi: 2, y_lo: 2; y = y_hi * 2 + y_lo), z: 8, core: 2. Of those that a mesh axis runs over, the one named last changes fastest.
Arguments:
- features: bfloat16 [1024, 512, 128], P('row', 'col'), may hold values from -6 to 6
- cotangent: bfloat16 [1024, 512, 128], P('row', 'col'), may hold values from -6 to 6
- kernels: bfloat16 [2, 9, 128, 128], replicated, may hold values from -0.1875 to 0.1875
- momentum: float32 [2, 147456], replicated, may hold values from -6 to 6
- mlp_in_weight: float32 [32, 3], replicated, may hold values from -3.5 to 3.5
- mlp_in_bias: float32 [32], replicated, may hold values from -3 to 3
- mlp_out_weight: float32 [2, 32], replicated, may hold values from -1 to 1
- mlp_out_bias: float32 [2], replicated, may hold values from -3 to 3
Outputs:
- update: float32 [2, 147456], replicated
- momentum_out: float32 [2, 147456], replicated
All inputs are finite; a program needn't handle non-finite values.
Results may differ from a plain program's by a relative error of at most 0.0014.
Values may be sent and summed in bfloat16 or wider, within the bound.
No kernel may reach another device: no remote copies, remote signals or barrier semaphores. Data moves between devices by JAX's collectives and lax.ppermute only.
A program may use at most 64 MiB of HBM per device.

v0:
```python
import math

import jax
import jax.numpy as jnp
from jax import lax
from jax.sharding import PartitionSpec as P


def padded_2(cells, sides, width):
    for axis, dim in sides:
        count = lax.axis_size(axis)
        head = lax.slice_in_dim(cells, 0, width, axis=dim)
        tail = lax.slice_in_dim(cells, cells.shape[dim] - width, cells.shape[dim], axis=dim)
        cells = jnp.concatenate(
            [
                lax.ppermute(tail, axis, [(i, (i + 1) % count) for i in range(count)]),
                cells,
                lax.ppermute(head, axis, [((i + 1) % count, i) for i in range(count)]),
            ],
            axis=dim,
        )
    return cells


def convolve(padded, kernel, tile_rows, tile_cols):
    channels = padded.shape[-1]
    summed = jnp.zeros((tile_rows * tile_cols, kernel.shape[-1]), jnp.float32)
    for tap_row in range(3):
        for tap_col in range(3):
            window = padded[tap_row : tap_row + tile_rows, tap_col : tap_col + tile_cols].reshape(
                tile_rows * tile_cols, channels
            )
            summed = summed + jnp.dot(
                window, kernel[3 * tap_row + tap_col], preferred_element_type=jnp.float32
            )
    return summed.reshape(tile_rows, tile_cols, -1)


def kernel_grad(padded, cotangent, tile_rows, tile_cols):
    channels = padded.shape[-1]
    flat_cot = cotangent.reshape(tile_rows * tile_cols, -1)
    taps = []
    for tap_row in range(3):
        for tap_col in range(3):
            window = padded[tap_row : tap_row + tile_rows, tap_col : tap_col + tile_cols].reshape(
                tile_rows * tile_cols, channels
            )
            taps.append(
                lax.dot_general(
                    window, flat_cot, (((0,), (0,)), ((), ())), preferred_element_type=jnp.float32
                )
            )
    return jnp.stack(taps)


def transpose_conv(cot_pad, kernel, tile_rows, tile_cols):
    channels = cot_pad.shape[-1]
    summed = jnp.zeros((tile_rows * tile_cols, kernel.shape[-2]), jnp.float32)
    for tap_row in range(3):
        for tap_col in range(3):
            window = cot_pad[
                2 - tap_row : 2 - tap_row + tile_rows, 2 - tap_col : 2 - tap_col + tile_cols
            ].reshape(tile_rows * tile_cols, channels)
            summed = summed + lax.dot_general(
                window,
                kernel[3 * tap_row + tap_col],
                (((1,), (1,)), ((), ())),
                preferred_element_type=jnp.float32,
            )
    return summed.reshape(tile_rows, tile_cols, -1)


def learned_step(grads, squares, momentum, weights, w_in, b_in, w_out, b_out, gain, count):
    norm_scale = 1.0 / jnp.sqrt(squares / count + 1e-06)
    g_hat = grads * norm_scale[:, None]
    momentum_new = 0.9 * momentum + 0.1 * g_hat
    scaled = weights.astype(jnp.float32) * gain
    pre_units = (
        w_in[:, 0][:, None, None] * g_hat[None] + w_in[:, 1][:, None, None] * momentum_new[None]
    )
    pre_units = pre_units + w_in[:, 2][:, None, None] * scaled[None] + b_in[:, None, None]
    units = jax.nn.silu(pre_units)
    mlp_result = (
        jnp.einsum("kh,hlp->klp", w_out, units, precision=lax.Precision.HIGHEST)
        + b_out[:, None, None]
    )
    update = mlp_result[0] * jnp.exp(jnp.tanh(mlp_result[1]))
    return (update, momentum_new)


def on_device(
    features, cotangent, kernels, momentum, mlp_in_weight, mlp_in_bias, mlp_out_weight, mlp_out_bias
):
    tile_rows, tile_cols, channels = features.shape
    param_count = 9 * channels * channels
    image_pad = padded_2(features, (("row", 0), ("col", 1)), 1)
    pre_act = convolve(image_pad, kernels[0], tile_rows, tile_cols)
    hidden = jax.nn.silu(pre_act).astype(jnp.bfloat16)
    hidden_pad = padded_2(hidden, (("row", 0), ("col", 1)), 1)
    cot_pad = padded_2(cotangent, (("row", 0), ("col", 1)), 1)
    grad_two = kernel_grad(hidden_pad, cotangent, tile_rows, tile_cols)
    back_grad = transpose_conv(cot_pad, kernels[1], tile_rows, tile_cols)
    sigma_val = jax.nn.sigmoid(pre_act)
    pre_grad = (back_grad * sigma_val * (1.0 + pre_act * (1.0 - sigma_val))).astype(jnp.bfloat16)
    grad_one = kernel_grad(image_pad, pre_grad, tile_rows, tile_cols)
    local_grads = jnp.stack([grad_one.reshape(-1), grad_two.reshape(-1)])
    weights = kernels.reshape(2, param_count)
    gain = math.sqrt(9.0 * channels)
    grads = lax.psum(local_grads, ("row", "col"))
    squares = jnp.sum(grads * grads, axis=1)
    update, momentum_out = learned_step(
        grads,
        squares,
        momentum,
        weights,
        mlp_in_weight,
        mlp_in_bias,
        mlp_out_weight,
        mlp_out_bias,
        gain,
        float(param_count),
    )
    return (update, momentum_out)


def solution(mesh):
    placed = (P("row", "col", None), P("row", "col", None), P(), P(), P(), P(), P(), P())
    return jax.shard_map(
        on_device, mesh=mesh, in_specs=placed, out_specs=(P(), P()), check_vma=False
    )
```

profile of v0, /device:TPU:6, one launch (start us, length us, event | category | flops | bytes accessed | tf_op | source)
XLA Modules:
  0.0 377.5 jit_solution(3197987723438845641)
XLA Ops:
  7.2 1.3 copy.30
  8.7 1.7 collective-permute-start.1
  10.4 0.7 fusion.119
  11.1 1.7 collective-permute-start.4
  12.9 3.3 collective-permute-start.2
  16.2 5.4 %collective-permute-start.7 = (bf16[66,1,128]{2,0,1:T(8,128)(2,1)S(1)}, bf16[66,1,128]{2,0,1:T(8,128)(2,1)S(1)}, u32[]{:S(2)}, u32[]{:S(2)}) collective-permute-start(bf16[66,1,128]{2,0,1:T(8,128)(2,1)S(1)} %get-tuple-element.24), channel_id=1, source_target_pairs={{1,0},{2,1},{3,2},{4,3},{5,4},{6,5},{7,6},{8,7},{9,8},{10,9},{11,1... | collective-permute-start | bytes 50696 | tf_op jit(solution)/shard_map/ppermute | solution.py:18
  21.9 0.3 fusion.75
  22.2 0.3 fusion.68
  22.5 0.4 pad_maximum_fusion.7
  22.9 0.3 copy.35
  23.2 0.3 copy.41
  23.6 3.5 collective-permute-start.5
  27.4 0.3 pad_maximum_fusion.1
  27.7 0.6 fusion.116
  28.3 0.3 copy.33
  29.0 0.3 copy.36
  29.3 0.3 copy.37
  29.7 0.3 copy.38
  30.0 0.3 copy.39
  30.4 0.3 copy.42
  30.7 4.1 %collective-permute-done.6 = bf16[66,1,128]{2,1,0:T(2,128)(2,1)S(1)} collective-permute-done((bf16[66,1,128]{2,1,0:T(2,128)(2,1)S(1)}, bf16[66,1,128]{2,1,0:T(2,128)(2,1)S(1)}, u32[]{:S(2)}, u32[]{:S(2)}) %collective-permute-start.6) | collective-permute-done | bytes 16928 | tf_op jit(solution)/shard_map/ppermute | solution.py:16
  34.8 0.7 pad_maximum_fusion.11
  35.5 0.3 fusion.66
  36.7 0.7 copy-done.4
  38.9 0.3 convolution_add_fusion.14
  39.2 0.3 convolution_add_fusion.13
  39.5 0.3 convolution_add_fusion.12
  39.8 0.3 convolution_add_fusion.11
  40.1 0.3 convolution_add_fusion.10
  40.4 0.4 fusion.21
  40.7 1.4 fusion.43
  42.1 0.3 fusion.41
  42.5 0.3 fusion.40
  42.8 0.3 fusion.39
  43.2 0.3 fusion.38
  43.5 0.4 fusion.37
  43.9 0.3 fusion.36
  44.3 0.3 fusion.35
  44.7 1.9 collective-permute-start.8
  46.5 0.4 collective-permute-start.9
  46.9 0.3 fusion.34
  47.3 0.6 collective-permute-done.8
  47.9 2.8 collective-permute-done.9
  50.9 5.6 %collective-permute-start.11 = (bf16[66,1,128]{2,0,1:T(8,128)(2,1)S(1)}, bf16[66,1,128]{2,0,1:T(8,128)(2,1)S(1)}, u32[]{:S(2)}, u32[]{:S(2)}) collective-permute-start(bf16[66,1,128]{2,0,1:T(8,128)(2,1)S(1)} %get-tuple-element.20), channel_id=1, source_target_pairs={{1,0},{2,1},{3,2},{4,3},{5,4},{6,5},{7,6},{8,7},{9,8},{10,9},{11,1... | collective-permute-start | bytes 50696 | tf_op jit(solution)/shard_map/ppermute | solution.py:18
  56.5 0.3 fusion.33
  56.9 1.4 collective-permute-done.10
  58.2 0.4 pad_maximum_fusion.2
  58.6 0.4 fusion.32
  59.0 0.5 fusion.31
  59.5 0.4 fusion.30
  59.9 0.4 fusion.29
  60.3 0.4 fusion.28
  60.7 0.4 fusion.27
  61.1 0.4 fusion.26
  61.6 0.5 fusion.25
  62.1 0.4 fusion.24
  62.5 1.9 pad_maximum_fusion
  64.6 4.3 %copy.91 = f32[1,2,1152,128]{3,1,2,0:T(2,128)S(1)} copy(f32[1,2,1152,128]{3,2,1,0:T(8,128)S(1)} %bitcast.218) | data formatting | bytes 2359296
  68.9 258.7 %all-reduce.2.cloned.1.call-done = f32[2,147456]{1,0:T(2,128)} async-done(((f32[2,147456]{1,0:T(2,128)}), f32[2,147456]{1,0:T(2,128)}) %all-reduce.2.cloned.1.call-update) | async-done | bytes 1179664 | tf_op jit(solution)/shard_map/psum | solution.py:109
  327.7 2.5 multiply_reduce_fusion
  330.2 1.3 multiply_add_fusion
  331.6 33.7 %fusion = f32[2,2,147456]{2,0,1:T(2,128)S(1)} fusion(f32[32]{0:T(128)S(1)} %copy-done.8, f32[2,147456]{1,0:T(2,128)S(1)} %bitcast.239, f32[32]{0:T(128)S(1)} %get-tuple-element.43, f32[2,147456]{1,0:T(2,128)S(1)} %get-tuple-element.2, f32[32]{0:T(128)S(1)} %get-tuple-element.44, f32[2,147456]{1,0:T(2,128)S(1)} %get-tuple-element.3, ...), kind=kOutput, calls=%fused_computation.1 | convolution fusion | flops 321454080 | bytes 5899016 | tf_op jit(solution)/shard_map/kh,hlp->klp/dot_general | solution.py:84
  365.3 2.5 fusion.23
  367.8 2.7 copy.92
  (53 shorter events, 3.6 us)
Async XLA Ops:
  7.2 324.4 %copy-start = (f32[2,32]{1,0:T(2,128)S(1)}, f32[2,32]{1,0:T(2,128)}, u32[]{:S(2)}) copy-start(f32[2,32]{1,0:T(2,128)} %param.14) | copy-start | bytes 772
  7.2 14.4 %copy-start.3 = (bf16[64,32,128]{2,1,0:T(8,128)(2,1)S(1)}, bf16[64,32,128]{2,1,0:T(8,128)(2,1)}, u32[]{:S(2)}) copy-start(bf16[64,32,128]{2,1,0:T(8,128)(2,1)} %param.9) | copy-start | bytes 1572868
  7.2 320.5 %all-reduce.2.cloned.1.call-start = ((), (), s32[]{:S(2)}) async-start(), calls=%async_computation | async-start | bytes 2359296 | tf_op jit(solution)/shard_map/psum | solution.py:109
  8.6 4.3 %collective-permute-start = (bf16[1,32,128]{2,0,1:T(2,128)(2,1)S(1)}, bf16[1,32,128]{2,0,1:T(2,128)(2,1)S(1)}, u32[]{:S(2)}, u32[]{:S(2)}) collective-permute-start(bf16[1,32,128]{2,0,1:T(2,128)(2,1)S(1)} %get-tuple-element.40), channel_id=1, source_target_pairs={{0,16},{16,32},{32,48},{48,64},{64,80},{80,96},{96,112},{112,128},... | collective-permute-start | bytes 24584 | tf_op jit(solution)/shard_map/ppermute | solution.py:16
  8.7 4.2 %collective-permute-start.1 = (bf16[1,32,128]{2,0,1:T(2,128)(2,1)S(1)}, bf16[1,32,128]{2,0,1:T(2,128)(2,1)S(1)}, u32[]{:S(2)}, u32[]{:S(2)}) collective-permute-start(bf16[1,32,128]{2,0,1:T(2,128)(2,1)S(1)} %get-tuple-element.41), channel_id=1, source_target_pairs={{16,0},{32,16},{48,32},{64,48},{80,64},{96,80},{112,96},{128,112},... | collective-permute-start | bytes 24584 | tf_op jit(solution)/shard_map/ppermute | solution.py:18
  11.1 10.4 %collective-permute-start.3 = (bf16[1,32,128]{2,1,0:T(8,128)(2,1)S(1)}, bf16[1,32,128]{2,1,0:T(8,128)(2,1)S(1)}, u32[]{:S(2)}, u32[]{:S(2)}) collective-permute-start(bf16[1,32,128]{2,1,0:T(8,128)(2,1)S(1)} %get-tuple-element.35), channel_id=1, source_target_pairs={{0,16},{16,32},{32,48},{48,64},{64,80},{80,96},{96,112},{112,128},... | collective-permute-start | bytes 24584 | tf_op jit(solution)/shard_map/ppermute | solution.py:16
  11.1 10.4 %collective-permute-start.4 = (bf16[1,32,128]{2,1,0:T(8,128)(2,1)S(1)}, bf16[1,32,128]{2,1,0:T(8,128)(2,1)S(1)}, u32[]{:S(2)}, u32[]{:S(2)}) collective-permute-start(bf16[1,32,128]{2,1,0:T(8,128)(2,1)S(1)} %get-tuple-element.34), channel_id=1, source_target_pairs={{16,0},{32,16},{48,32},{64,48},{80,64},{96,80},{112,96},{128,112},... | collective-permute-start | bytes 24584 | tf_op jit(solution)/shard_map/ppermute | solution.py:18
  12.9 9.0 %copy-start.2 = (bf16[2,9,128,128]{3,2,1,0:T(8,128)(2,1)S(1)}, bf16[2,9,128,128]{3,2,1,0:T(8,128)(2,1)}, u32[]{:S(2)}) copy-start(bf16[2,9,128,128]{3,2,1,0:T(8,128)(2,1)} %param.10) | copy-start | bytes 1769476
  12.9 14.5 %collective-permute-start.2 = (bf16[66,1,128]{2,0,1:T(8,128)(2,1)S(1)}, bf16[66,1,128]{2,0,1:T(8,128)(2,1)S(1)}, u32[]{:S(2)}, u32[]{:S(2)}) collective-permute-start(bf16[66,1,128]{2,0,1:T(8,128)(2,1)S(1)} %get-tuple-element.25), channel_id=1, source_target_pairs={{0,1},{1,2},{2,3},{3,4},{4,5},{5,6},{6,7},{7,8},{8,9},{9,10},{10,1... | collective-permute-start | bytes 50696 | tf_op jit(solution)/shard_map/ppermute | solution.py:16
  16.2 11.2 %collective-permute-start.7 = (bf16[66,1,128]{2,0,1:T(8,128)(2,1)S(1)}, bf16[66,1,128]{2,0,1:T(8,128)(2,1)S(1)}, u32[]{:S(2)}, u32[]{:S(2)}) collective-permute-start(bf16[66,1,128]{2,0,1:T(8,128)(2,1)S(1)} %get-tuple-element.24), channel_id=1, source_target_pairs={{1,0},{2,1},{3,2},{4,3},{5,4},{6,5},{7,6},{8,7},{9,8},{10,9},{11,1... | collective-permute-start | bytes 50696 | tf_op jit(solution)/shard_map/ppermute | solution.py:18
  23.6 7.1 %collective-permute-start.5 = (bf16[66,1,128]{2,1,0:T(2,128)(2,1)S(1)}, bf16[66,1,128]{2,1,0:T(2,128)(2,1)S(1)}, u32[]{:S(2)}, u32[]{:S(2)}) collective-permute-start(bf16[66,1,128]{2,1,0:T(2,128)(2,1)S(1)} %get-tuple-element.29), channel_id=1, source_target_pairs={{1,0},{2,1},{3,2},{4,3},{5,4},{6,5},{7,6},{8,7},{9,8},{10,9},{11,1... | collective-permute-start | bytes 50696 | tf_op jit(solution)/shard_map/ppermute | solution.py:18
  27.1 7.7 %collective-permute-start.6 = (bf16[66,1,128]{2,1,0:T(2,128)(2,1)S(1)}, bf16[66,1,128]{2,1,0:T(2,128)(2,1)S(1)}, u32[]{:S(2)}, u32[]{:S(2)}) collective-permute-start(bf16[66,1,128]{2,1,0:T(2,128)(2,1)S(1)} %get-tuple-element.30), channel_id=1, source_target_pairs={{0,1},{1,2},{2,3},{3,4},{4,5},{5,6},{6,7},{7,8},{8,9},{9,10},{10,1... | collective-permute-start | bytes 50696 | tf_op jit(solution)/shard_map/ppermute | solution.py:16
  36.4 1.0 copy-start.4
  44.7 3.2 collective-permute-start.8
  46.5 4.2 %collective-permute-start.9 = (bf16[1,32,128]{2,0,1:T(2,128)(2,1)S(1)}, bf16[1,32,128]{2,0,1:T(2,128)(2,1)S(1)}, u32[]{:S(2)}, u32[]{:S(2)}) collective-permute-start(bf16[1,32,128]{2,0,1:T(2,128)(2,1)S(1)} %get-tuple-element.37), channel_id=1, source_target_pairs={{16,0},{32,16},{48,32},{64,48},{80,64},{96,80},{112,96},{128,112},... | collective-permute-start | bytes 24584 | tf_op jit(solution)/shard_map/ppermute | solution.py:18
  50.8 7.5 %collective-permute-start.10 = (bf16[66,1,128]{2,0,1:T(8,128)(2,1)S(1)}, bf16[66,1,128]{2,0,1:T(8,128)(2,1)S(1)}, u32[]{:S(2)}, u32[]{:S(2)}) collective-permute-start(bf16[66,1,128]{2,0,1:T(8,128)(2,1)S(1)} %get-tuple-element.21), channel_id=1, source_target_pairs={{0,1},{1,2},{2,3},{3,4},{4,5},{5,6},{6,7},{7,8},{8,9},{9,10},{10,1... | collective-permute-start | bytes 50696 | tf_op jit(solution)/shard_map/ppermute | solution.py:16
  50.9 7.4 %collective-permute-start.11 = (bf16[66,1,128]{2,0,1:T(8,128)(2,1)S(1)}, bf16[66,1,128]{2,0,1:T(8,128)(2,1)S(1)}, u32[]{:S(2)}, u32[]{:S(2)}) collective-permute-start(bf16[66,1,128]{2,0,1:T(8,128)(2,1)S(1)} %get-tuple-element.20), channel_id=1, source_target_pairs={{1,0},{2,1},{3,2},{4,3},{5,4},{6,5},{7,6},{8,7},{9,8},{10,9},{11,1... | collective-permute-start | bytes 50696 | tf_op jit(solution)/shard_map/ppermute | solution.py:18
  64.6 4.3 %copy-start.7 = (f32[32,3]{0,1:T(4,128)S(1)}, f32[32,3]{0,1:T(4,128)}, u32[]{:S(2)}) copy-start(f32[32,3]{0,1:T(4,128)} %param.12) | copy-start | bytes 1156
  64.6 265.6 %copy-start.5 = (f32[2,147456]{1,0:T(2,128)S(1)}, f32[2,147456]{1,0:T(2,128)}, u32[]{:S(2)}) copy-start(f32[2,147456]{1,0:T(2,128)} %param.11) | copy-start | bytes 3538948
  327.7 2.5 copy-start.1
  330.2 1.4 copy-start.8
  330.2 1.4 copy-start.9
  331.6 33.7 %copy-start.6 = (f32[2,147456]{1,0:T(2,128)}, f32[2,147456]{1,0:T(2,128)S(1)}, u32[]{:S(2)}) copy-start(f32[2,147456]{1,0:T(2,128)S(1)} %get-tuple-element.2) | copy-start | bytes 3538948
Sparse Core Ops, SparseCore 0:
  64.6 263.0 all-reduce.1
where the time goes:
time: 384 us; the launch traced here: 378 us
  waiting for transfers between devices  268 us (70%)
  matrix products  45.9 us (12%)
  starting transfers between devices  24 us (6%)
  between operations  14.8 us (4%)
  local copies, waits for them, and re-layouts  13.3 us (3%)
  other arithmetic  11.9 us (3%)
    psum x1, waiting for transfers between devices, on_device(): grads = lax.psum(local_grads, ('row', 'col'))  259 us
    dot_general x1, matrix products, learned_step(): jnp.einsum('kh,hlp->klp', w_out, units, precision=lax.Precision.HIGHEST)  33.7 us
    ppermute x6, starting transfers between devices, padded_2(): lax.ppermute(head, axis, [((i + 1) % count, i) for i in range(count)])  18.4 us
    unnamed x24, local copies, waits for them, and re-layouts  9.07 us
  transfers between devices with their start and end apart: 13, of which 5 were waited for; matrix products, arithmetic and copies ran while one was open for 3% of the time, Pallas kernels for 0%

commit v1 on v0

v1 whole, which is shorter than its diff:
```python
import math

import jax
import jax.numpy as jnp
from jax import lax
from jax.sharding import PartitionSpec as P

AXES = ("row", "col")


def flat_index(x, y, z, core):
    return (((y % 2) * 4 + x) * 2 + core) * 16 + z * 2 + y // 2


COORDS = [(x, y, z, c) for y in range(4) for x in range(4) for z in range(8) for c in range(2)]


def pairs_of(fn):
    return [(flat_index(*p), flat_index(*fn(*p))) for p in COORDS]


CORE_PAIRS = pairs_of(lambda x, y, z, c: (x, y, z, 1 - c))
Z_TABLES = ((1, 0, 3, 2, 5, 4, 7, 6), (7, 2, 1, 4, 3, 6, 5, 0), (3, 6, 5, 0, 7, 2, 1, 4))
Z_PAIRS = [pairs_of(lambda x, y, z, c, t=t: (x, y, t[z], c)) for t in Z_TABLES]
PLANES = [
    [flat_index(x, y, z, c) for y in range(4) for x in range(4)] for z in range(8) for c in range(2)
]


def padded_2(cells, sides, width):
    for axis, dim in sides:
        count = lax.axis_size(axis)
        head = lax.slice_in_dim(cells, 0, width, axis=dim)
        tail = lax.slice_in_dim(cells, cells.shape[dim] - width, cells.shape[dim], axis=dim)
        cells = jnp.concatenate(
            [
                lax.ppermute(tail, axis, [(i, (i + 1) % count) for i in range(count)]),
                cells,
                lax.ppermute(head, axis, [((i + 1) % count, i) for i in range(count)]),
            ],
            axis=dim,
        )
    return cells


def window_of(padded, row, col, tile_rows, tile_cols):
    return padded[row : row + tile_rows, col : col + tile_cols].reshape(
        tile_rows * tile_cols, padded.shape[-1]
    )


def convolve(padded, kernel, tile_rows, tile_cols):
    summed = jnp.zeros((tile_rows * tile_cols, kernel.shape[-1]), jnp.float32)
    for tap in range(9):
        window = window_of(padded, tap // 3, tap % 3, tile_rows, tile_cols)
        summed = summed + jnp.dot(window, kernel[tap], preferred_element_type=jnp.float32)
    return summed


def transpose_conv(cot_pad, kernel, tile_rows, tile_cols):
    summed = jnp.zeros((tile_rows * tile_cols, kernel.shape[-2]), jnp.float32)
    for tap in range(9):
        window = window_of(cot_pad, 2 - tap // 3, 2 - tap % 3, tile_rows, tile_cols)
        summed = summed + lax.dot_general(
            window, kernel[tap], (((1,), (1,)), ((), ())), preferred_element_type=jnp.float32
        )
    return summed


def outer(left, right):
    return lax.dot_general(left, right, (((0,), (0,)), ((), ())), preferred_element_type=jnp.float32)


def on_device(
    features, cotangent, kernels, momentum, mlp_in_weight, mlp_in_bias, mlp_out_weight, mlp_out_bias
):
    tile_rows, tile_cols, channels = features.shape
    lines = 9 * channels
    core = lax.axis_index("row") % 2
    both = padded_2(jnp.stack([features, cotangent]), (("row", 1), ("col", 2)), 1)
    image_pad, cot_pad = both[0], both[1]
    pre_act = convolve(image_pad, kernels[0], tile_rows, tile_cols)
    hidden = jax.nn.silu(pre_act).astype(jnp.bfloat16)
    grad_two = jnp.concatenate(
        [
            outer(hidden, window_of(cot_pad, 2 - tap // 3, 2 - tap % 3, tile_rows, tile_cols))
            for tap in range(9)
        ]
    )
    back_grad = transpose_conv(cot_pad, kernels[1], tile_rows, tile_cols)
    sigma = jax.nn.sigmoid(pre_act)
    pre_grad = (back_grad * sigma * (1.0 + pre_act * (1.0 - sigma))).astype(jnp.bfloat16)
    grad_one = jnp.concatenate(
        [
            outer(window_of(image_pad, tap // 3, tap % 3, tile_rows, tile_cols), pre_grad)
            for tap in range(9)
        ]
    )
    first = core == 0
    mine = jnp.where(first, grad_one, grad_two)
    other = jnp.where(first, grad_two, grad_one)
    mine = mine + lax.ppermute(other, AXES, CORE_PAIRS)
    parts = lax.all_to_all(
        mine.reshape(16, lines // 16, channels), AXES, 0, 0, axis_index_groups=PLANES, tiled=True
    )
    part = jnp.sum(parts, axis=0)
    for pairs in Z_PAIRS:
        part = part + lax.ppermute(part, AXES, pairs)
    grads = lax.all_to_all(
        jnp.broadcast_to(part[None], parts.shape), AXES, 0, 0, axis_index_groups=PLANES, tiled=True
    ).reshape(lines, channels)

    count = float(lines * channels)
    pick = lambda a: jnp.where(first, a[0], a[1])
    scaled = pick(kernels.reshape(2, lines, channels)).astype(jnp.float32) * math.sqrt(9.0 * channels)
    g_hat = grads / jnp.sqrt(jnp.sum(grads * grads) / count + 1e-06)
    momentum_new = 0.9 * pick(momentum.reshape(2, lines, channels)) + 0.1 * g_hat
    top = jnp.zeros_like(g_hat)
    low = jnp.zeros_like(g_hat)
    for h in range(mlp_in_bias.shape[0]):
        pre = mlp_in_weight[h, 0] * g_hat + mlp_in_weight[h, 1] * momentum_new
        unit = jax.nn.silu(pre + mlp_in_weight[h, 2] * scaled + mlp_in_bias[h])
        top = top + mlp_out_weight[0, h] * unit
        low = low + mlp_out_weight[1, h] * unit
    update = (top + mlp_out_bias[0]) * jnp.exp(jnp.tanh(low + mlp_out_bias[1]))
    outs = []
    for value in (update, momentum_new):
        theirs = lax.ppermute(value, AXES, CORE_PAIRS)
        pair = jnp.stack([jnp.where(first, value, theirs), jnp.where(first, theirs, value)])
        outs.append(pair.reshape(2, lines * channels))
    return tuple(outs)


def solution(mesh):
    placed = (P("row", "col", None), P("row", "col", None), P(), P(), P(), P(), P(), P())
    return jax.shard_map(
        on_device, mesh=mesh, in_specs=placed, out_specs=(P(), P()), check_vma=False
    )
```

time: 384 us -> 232 us (0.60)
  the two profiles are of different devices: /device:TPU:6 before, /device:TPU:1 now
where the time goes in v1:
time: 232 us; the launch traced here: 230 us
  other arithmetic  139 us (60%)
  starting transfers between devices  39.3 us (17%)
  between operations  21.9 us (9%)
  local copies, waits for them, and re-layouts  14.2 us (6%)
  matrix products  11.8 us (5%)
  waiting for transfers between devices  4.21 us (2%)
    mul x1, other arithmetic, on_device(): update = (top + mlp_out_bias[0]) * jnp.exp(jnp.tanh(low + mlp_out_bias[1]))  93.5 us
    mul x1, other arithmetic, on_device(): pre = mlp_in_weight[h, 0] * g_hat + mlp_in_weight[h, 1] * momentum_new  13.5 us
    mul x1, other arithmetic, on_device(): 0.1 * g_hat  13.1 us
    ppermute x3, starting transfers between devices, on_device(): part = part + lax.ppermute(part, AXES, pairs)  9.71 us
    mul x3, other arithmetic, on_device(): unit = jax.nn.silu(pre + mlp_in_weight[h, 2] * scaled + mlp_in_bias[h])  7.5 us
    all_to_all x1, starting transfers between devices, on_device(): lax.all_to_all(jnp.broadcast_to(part[None], parts.shape), AXES, 0, 0, axi...  6.65 us
    ppermute x2, starting transfers between devices, padded_2(): lax.ppermute(head, axis, [((i + 1) % count, i) for i in range(count)])  6.24 us
    dot_general x18, matrix products, outer(): lax.dot_general(left, right, (((0,), (0,)), ((), ())), preferred_element_...  6.2 us
  transfers between devices with their start and end apart: 12, of which 5 were waited for; matrix products, arithmetic and copies ran while one was open for 10% of the time, Pallas kernels for 0%

profile of v1, /device:TPU:1, one launch (start us, length us, event | category | flops | bytes accessed | tf_op | source)
XLA Modules:
  0.0 229.8 jit_solution(5139402694090382202)
XLA Ops:
  0.7 0.8 pad_maximum_fusion.8
  1.5 2.6 %collective-permute-start = (bf16[2,1,32,128]{3,2,1,0:T(8,128)(2,1)S(1)}, bf16[2,1,32,128]{3,2,1,0:T(8,128)(2,1)S(1)}, u32[]{:S(2)}, u32[]{:S(2)}) collective-permute-start(bf16[2,1,32,128]{3,2,1,0:T(8,128)(2,1)S(1)} %get-tuple-element.14), channel_id=1, source_target_pairs={{0,16},{16,32},{32,48},{48,64},{64,80},{80,96},{96,112},{112,128},... | collective-permute-start | bytes 49160 | tf_op jit(solution)/shard_map/ppermute | solution.py:37
  4.1 0.7 collective-permute-start.1
  4.8 2.1 fusion.79
  6.9 3.4 %fusion.3 = f32[1,147456]{1,0:T(1,128)} fusion(pred[]{:T(512)S(6)} %eq.5, f32[2,147456]{1,0:T(2,128)} %param.11), kind=kLoop, calls=%fused_computation.77 | loop fusion | flops 294912 | bytes 1769473 | tf_op jit(solution)/shard_map/mul | solution.py:117
  10.3 0.7 fusion.80
  11.2 2.3 %collective-permute-start.2 = (bf16[2,66,1,128]{3,2,1,0:T(2,128)(2,1)S(1)}, bf16[2,66,1,128]{3,2,1,0:T(2,128)(2,1)S(1)}, u32[]{:S(2)}, u32[]{:S(2)}) collective-permute-start(bf16[2,66,1,128]{3,2,1,0:T(2,128)(2,1)S(1)} %get-tuple-element.12), channel_id=1, source_target_pairs={{0,1},{1,2},{2,3},{3,4},{4,5},{5,6},{6,7},{7,8},{8,9},{9,10},{10,1... | collective-permute-start | bytes 101384 | tf_op jit(solution)/shard_map/ppermute | solution.py:37
  13.5 5.6 %collective-permute-start.3 = (bf16[2,66,1,128]{3,2,1,0:T(2,128)(2,1)S(1)}, bf16[2,66,1,128]{3,2,1,0:T(2,128)(2,1)S(1)}, u32[]{:S(2)}, u32[]{:S(2)}) collective-permute-start(bf16[2,66,1,128]{3,2,1,0:T(2,128)(2,1)S(1)} %get-tuple-element.13), channel_id=1, source_target_pairs={{1,0},{2,1},{3,2},{4,3},{5,4},{6,5},{7,6},{8,7},{9,8},{10,9},{11,1... | collective-permute-start | bytes 101384 | tf_op jit(solution)/shard_map/ppermute | solution.py:39
  19.1 0.7 fusion.82
  20.5 0.8 pad_maximum_fusion
  21.5 2.4 %fusion.74 = (bf16[64,32,128]{2,1,0:T(8,128)(2,1)S(1)}, bf16[64,32,128]{2,1,0:T(8,128)(2,1)S(1)}, bf16[64,32,128]{2,1,0:T(8,128)(2,1)S(1)}, bf16[64,32,128]{2,1,...) fusion(bf16[66,34,128]{2,1,0:T(8,128)(2,1)S(1)} %get-tuple-elem, ...), kind=kLoop, calls=%fused_computation.262 | loop fusion | bytes 18874368 | tf_op jit(solution)/shard_map/slice | solution.py:47
  24.8 0.3 convolution_add_fusion.14
  28.6 0.4 multiply_convert_fusion
  29.1 0.6 fusion.2
  29.6 0.3 convolution_dynamic-update-slice_fusion.17
  30.0 0.4 convolution_dynamic-update-slice_fusion.16
  30.4 0.4 convolution_dynamic-update-slice_fusion.15
  30.7 0.4 convolution_dynamic-update-slice_fusion.14
  31.1 0.4 convolution_dynamic-update-slice_fusion.13
  31.4 0.4 convolution_dynamic-update-slice_fusion.12
  31.8 0.4 convolution_dynamic-update-slice_fusion.11
  32.1 0.4 convolution_dynamic-update-slice_fusion.10
  32.5 0.3 convolution_dynamic-update-slice_fusion.9
  32.8 0.3 convolution_dynamic-update-slice_fusion.8
  33.2 0.3 convolution_dynamic-update-slice_fusion.7
  33.5 0.3 convolution_dynamic-update-slice_fusion.6
  33.9 0.3 convolution_dynamic-update-slice_fusion.5
  34.2 0.3 convolution_dynamic-update-slice_fusion.4
  34.5 0.3 convolution_dynamic-update-slice_fusion.3
  34.9 0.3 convolution_dynamic-update-slice_fusion.2
  35.2 0.3 convolution_dynamic-update-slice_fusion.1
  35.6 0.4 convolution_dynamic-update-slice_fusion
  36.0 4.0 %collective-permute-start.4 = (f32[1152,128]{1,0:T(8,128)S(1)}, f32[1152,128]{1,0:T(8,128)S(1)}, u32[]{:S(2)}, u32[]{:S(2)}) collective-permute-start(f32[1152,128]{1,0:T(8,128)S(1)} %broadcast_select_fusion.5), channel_id=1, source_target_pairs={{0,16},{16,0},{2,18},{18,2},{4,20},{20,4},{6,22},{22,6},{8,24},{24... | collective-permute-start | bytes 1769480 | tf_op jit(solution)/shard_map/ppermute | solution.py:102
  40.0 0.7 fusion.81
  40.7 0.7 fusion.76
  41.4 0.7 fusion.77
  42.1 0.9 convert_multiply_fusion.31
  43.1 0.9 select_add_fusion
  44.0 3.6 %all-to-all-start = ((f32[16,72,128]{2,1,0:T(8,128)}), f32[16,72,128]{2,1,0:T(8,128)S(1)}, u32[]{:S(2)}, u32[]{:S(2)}) async-start(f32[16,72,128]{2,1,0:T(8,128)} %bitcast.42), calls=%async_computation | async-start | bytes 1179648 | tf_op jit(solution)/shard_map/all_to_all | solution.py:103
  47.6 0.7 fusion.83
  56.2 0.7 fusion.78
  56.9 2.5 %convert_multiply_fusion.12 = (f32[1,9,128,128]{3,2,1,0:T(8,128)S(1)}, f32[1,9,128,128]{3,2,1,0:T(8,128)S(1)}, f32[1,9,128,128]{3,2,1,0:T(8,128)S(1)}, f32[1,9,1...) fusion(bf16[1,9,128,128]{3,2,1,0:T(8,128)(2,1)S(1)} %get-tuple-, ...), kind=kLoop, calls=%fused_computation.12 | loop fusion | flops 2064384 | bytes 7962676 | tf_op jit(solution)/shard_map/mul | solution.py:122
  59.6 1.0 collective-permute-start.5
  60.6 0.7 fusion.85
  61.3 1.2 collective-permute-done.5
  62.5 3.9 %collective-permute-start.6 = (f32[72,128]{1,0:T(8,128)S(1)}, f32[72,128]{1,0:T(8,128)S(1)}, u32[]{:S(2)}, u32[]{:S(2)}) collective-permute-start(f32[72,128]{1,0:T(8,128)S(1)} %add.777), channel_id=1, source_target_pairs={{0,14},{16,30},{2,4},{18,20},{4,2},{20,18},{6,8},{22,24},{8,6},{24... | collective-permute-start | bytes 110600 | tf_op jit(solution)/shard_map/ppermute | solution.py:108
  66.4 0.7 fusion.86
  67.1 0.6 collective-permute-done.6
  67.8 4.8 %collective-permute-start.7 = (f32[72,128]{1,0:T(8,128)S(1)}, f32[72,128]{1,0:T(8,128)S(1)}, u32[]{:S(2)}, u32[]{:S(2)}) collective-permute-start(f32[72,128]{1,0:T(8,128)S(1)} %add.778), channel_id=1, source_target_pairs={{0,6},{16,22},{2,12},{18,28},{4,10},{20,26},{6,0},{22,16},{8,14},{... | collective-permute-start | bytes 110600 | tf_op jit(solution)/shard_map/ppermute | solution.py:108
  72.6 0.7 fusion.84
  73.2 0.7 collective-permute-done.7
  73.9 0.9 broadcast_in_dim.2
  74.8 6.7 %all-to-all-start.1 = ((f32[16,72,128]{2,1,0:T(8,128)}), f32[16,72,128]{2,1,0:T(8,128)S(1)}, u32[]{:S(2)}, u32[]{:S(2)}) async-start(f32[16,72,128]{2,1,0:T(8,128)} %broadcast_in_dim.2), calls=%async_computation.1 | async-start | bytes 1179648 | tf_op jit(solution)/shard_map/all_to_all | solution.py:109
  81.5 0.6 fusion.87
  82.1 0.6 slice.983
  93.9 4.1 %convert_multiply_fusion.30 = (f32[1,9,128,128]{3,2,1,0:T(8,128)}, f32[1,9,128,128]{3,2,1,0:T(8,128)}, f32[1,9,128,128]{3,2,1,0:T(8,128)}, f32[1,9,128,128]{3,2,...) fusion(bf16[1,9,128,128]{3,2,1,0:T(8,128)(2,1)S(1)} %get-tuple-, ...), kind=kLoop, calls=%fused_computation.30 | loop fusion | flops 2801664 | bytes 10911816 | tf_op jit(solution)/shard_map/mul | solution.py:122
  98.0 0.8 multiply_reduce_fusion
  99.5 13.5 %broadcast_multiply_fusion.32 = (f32[16,72,128]{2,1,0:T(8,128)}, f32[16,72,128]{2,1,0:T(8,128)}, f32[16,72,128]{2,1,0:T(8,128)}, f32[16,72,128]{2,1,0:T(8,128)},...) fusion(f32[]{:T(128)} %bitcast.1, ...), kind=kLoop, calls=%fused_computation.212 | loop fusion | flops 2359296 | bytes 9437248 | tf_op jit(solution)/shard_map/mul | solution.py:121
  113.3 13.1 %broadcast_multiply_fusion.31 = (f32[16,72,128]{2,1,0:T(8,128)S(1)}, f32[16,72,128]{2,1,0:T(8,128)S(1)}, f32[16,72,128]{2,1,0:T(8,128)S(1)}, f32[16,72,128]{2,1,...) fusion(f32[16,72,128]{2,1,0:T(8,128)S(1)} %all-to-all-done.1, ...), kind=kLoop, calls=%fused_computation.210 | loop fusion | flops 2801664 | bytes 11206728 | tf_op jit(solution)/shard_map/mul | solution.py:117
  126.6 93.5 %exponential_multiply_fusion = (f32[1152,128]{1,0:T(8,128)S(1)}, f32[1152,128]{1,0:T(8,128)S(1)}) fusion(f32[1,9,128,128]{3,2,1,0:T(8,128)S(1)} %copy-done.10, f32[16,72,128]{2,1,0:T(8,128)} %get-tuple-element.66, f32[1,9,128,128]{3,2,1,0:T(8,128)S(1)} %copy-done.9, f32[16,72,128]{2,1,0:T(8,128)} %get-tuple-element.65, f32[1,9,128,128]{3,2,1,0:T(8,128)S(1)} %copy-done.8, ...), kind=kLoop, calls=%fused_computation.175 | loop fusion | flops 56918016 | bytes 40108552 | tf_op jit(solution)/shard_map/mul | solution.py:125
  220.1 4.1 %collective-permute-start.8 = (f32[1152,128]{1,0:T(8,128)S(1)}, f32[1152,128]{1,0:T(8,128)S(1)}, u32[]{:S(2)}, u32[]{:S(2)}) collective-permute-start(f32[1152,128]{1,0:T(8,128)S(1)} %get-tuple-element.2), channel_id=1, source_target_pairs={{0,16},{16,0},{2,18},{18,2},{4,20},{20,4},{6,22},{22,6},{8,24},{24... | collective-permute-start | bytes 1769480 | tf_op jit(solution)/shard_map/ppermute | solution.py:128
  224.3 1.5 collective-permute-done.8
  225.9 1.9 pad_maximum_fusion.1
  227.9 1.9 pad_maximum_fusion.2
  (101 shorter events, 5.3 us)
Async XLA Ops:
  0.6 9.7 %copy-start.30 = (f32[32,3]{0,1:T(4,128)S(1)}, f32[32,3]{0,1:T(4,128)}, u32[]{:S(2)}) copy-start(f32[32,3]{0,1:T(4,128)} %param.12) | copy-start | bytes 1156
  0.6 10.4 %copy-start = (bf16[64,32,128]{2,1,0:T(8,128)(2,1)S(1)}, bf16[64,32,128]{2,1,0:T(8,128)(2,1)}, u32[]{:S(2)}) copy-start(bf16[64,32,128]{2,1,0:T(8,128)(2,1)} %param.9) | copy-start | bytes 1572868
  0.7 10.4 %copy-start.1 = (bf16[64,32,128]{2,1,0:T(8,128)(2,1)S(1)}, bf16[64,32,128]{2,1,0:T(8,128)(2,1)}, u32[]{:S(2)}) copy-start(bf16[64,32,128]{2,1,0:T(8,128)(2,1)} %param.8) | copy-start | bytes 1572868
  1.5 9.6 %collective-permute-start = (bf16[2,1,32,128]{3,2,1,0:T(8,128)(2,1)S(1)}, bf16[2,1,32,128]{3,2,1,0:T(8,128)(2,1)S(1)}, u32[]{:S(2)}, u32[]{:S(2)}) collective-permute-start(bf16[2,1,32,128]{3,2,1,0:T(8,128)(2,1)S(1)} %get-tuple-element.14), channel_id=1, source_target_pairs={{0,16},{16,32},{32,48},{48,64},{64,80},{80,96},{96,112},{112,128},... | collective-permute-start | bytes 49160 | tf_op jit(solution)/shard_map/ppermute | solution.py:37
  4.1 7.0 %collective-permute-start.1 = (bf16[2,1,32,128]{3,2,1,0:T(8,128)(2,1)S(1)}, bf16[2,1,32,128]{3,2,1,0:T(8,128)(2,1)S(1)}, u32[]{:S(2)}, u32[]{:S(2)}) collective-permute-start(bf16[2,1,32,128]{3,2,1,0:T(8,128)(2,1)S(1)} %get-tuple-element.15), channel_id=1, source_target_pairs={{16,0},{32,16},{48,32},{64,48},{80,64},{96,80},{112,96},{128,112},... | collective-permute-start | bytes 49160 | tf_op jit(solution)/shard_map/ppermute | solution.py:39
  6.9 12.2 %copy-start.31 = (f32[2,32]{1,0:T(2,128)S(1)}, f32[2,32]{1,0:T(2,128)}, u32[]{:S(2)}) copy-start(f32[2,32]{1,0:T(2,128)} %param.14) | copy-start | bytes 772
  11.2 9.3 %collective-permute-start.2 = (bf16[2,66,1,128]{3,2,1,0:T(2,128)(2,1)S(1)}, bf16[2,66,1,128]{3,2,1,0:T(2,128)(2,1)S(1)}, u32[]{:S(2)}, u32[]{:S(2)}) collective-permute-start(bf16[2,66,1,128]{3,2,1,0:T(2,128)(2,1)S(1)} %get-tuple-element.12), channel_id=1, source_target_pairs={{0,1},{1,2},{2,3},{3,4},{4,5},{5,6},{6,7},{7,8},{8,9},{9,10},{10,1... | collective-permute-start | bytes 101384 | tf_op jit(solution)/shard_map/ppermute | solution.py:37
  13.5 7.0 %collective-permute-start.3 = (bf16[2,66,1,128]{3,2,1,0:T(2,128)(2,1)S(1)}, bf16[2,66,1,128]{3,2,1,0:T(2,128)(2,1)S(1)}, u32[]{:S(2)}, u32[]{:S(2)}) collective-permute-start(bf16[2,66,1,128]{3,2,1,0:T(2,128)(2,1)S(1)} %get-tuple-element.13), channel_id=1, source_target_pairs={{1,0},{2,1},{3,2},{4,3},{5,4},{6,5},{7,6},{8,7},{9,8},{10,9},{11,1... | collective-permute-start | bytes 101384 | tf_op jit(solution)/shard_map/ppermute | solution.py:39
  21.5 2.4 %copy-start.29 = (bf16[2,9,128,128]{3,2,1,0:T(8,128)(2,1)S(1)}, bf16[2,9,128,128]{3,2,1,0:T(8,128)(2,1)}, u32[]{:S(2)}) copy-start(bf16[2,9,128,128]{3,2,1,0:T(8,128)(2,1)} %param.10) | copy-start | bytes 1769476
  36.0 7.1 %collective-permute-start.4 = (f32[1152,128]{1,0:T(8,128)S(1)}, f32[1152,128]{1,0:T(8,128)S(1)}, u32[]{:S(2)}, u32[]{:S(2)}) collective-permute-start(f32[1152,128]{1,0:T(8,128)S(1)} %broadcast_select_fusion.5), channel_id=1, source_target_pairs={{0,16},{16,0},{2,18},{18,2},{4,20},{20,4},{6,22},{22,6},{8,24},{24... | collective-permute-start | bytes 1769480 | tf_op jit(solution)/shard_map/ppermute | solution.py:102
  44.0 15.6 %all-to-all-start = ((f32[16,72,128]{2,1,0:T(8,128)}), f32[16,72,128]{2,1,0:T(8,128)S(1)}, u32[]{:S(2)}, u32[]{:S(2)}) async-start(f32[16,72,128]{2,1,0:T(8,128)} %bitcast.42), calls=%async_computation | async-start | bytes 1179648 | tf_op jit(solution)/shard_map/all_to_all | solution.py:103
  56.9 3.6 %copy-start.32 = (f32[32]{0:T(128)S(1)}, f32[32]{0:T(128)}, u32[]{:S(2)}) copy-start(f32[32]{0:T(128)} %param.13) | copy-start | bytes 388
  59.4 22.0 %copy-start.33 = (f32[2]{0:T(128)S(1)}, f32[2]{0:T(128)}, u32[]{:S(2)}) copy-start(f32[2]{0:T(128)} %param.15) | copy-start | bytes 28
  59.6 2.9 %collective-permute-start.5 = (f32[72,128]{1,0:T(8,128)S(1)}, f32[72,128]{1,0:T(8,128)S(1)}, u32[]{:S(2)}, u32[]{:S(2)}) collective-permute-start(f32[72,128]{1,0:T(8,128)S(1)} %reduce_sum.18), channel_id=1, source_target_pairs={{0,2},{16,18},{2,0},{18,16},{4,6},{20,22},{6,4},{22,20},{8,10},{24... | collective-permute-start | bytes 110600 | tf_op jit(solution)/shard_map/ppermute | solution.py:108
  62.5 5.3 %collective-permute-start.6 = (f32[72,128]{1,0:T(8,128)S(1)}, f32[72,128]{1,0:T(8,128)S(1)}, u32[]{:S(2)}, u32[]{:S(2)}) collective-permute-start(f32[72,128]{1,0:T(8,128)S(1)} %add.777), channel_id=1, source_target_pairs={{0,14},{16,30},{2,4},{18,20},{4,2},{20,18},{6,8},{22,24},{8,6},{24... | collective-permute-start | bytes 110600 | tf_op jit(solution)/shard_map/ppermute | solution.py:108
  67.8 6.2 %collective-permute-start.7 = (f32[72,128]{1,0:T(8,128)S(1)}, f32[72,128]{1,0:T(8,128)S(1)}, u32[]{:S(2)}, u32[]{:S(2)}) collective-permute-start(f32[72,128]{1,0:T(8,128)S(1)} %add.778), channel_id=1, source_target_pairs={{0,6},{16,22},{2,12},{18,28},{4,10},{20,26},{6,0},{22,16},{8,14},{... | collective-permute-start | bytes 110600 | tf_op jit(solution)/shard_map/ppermute | solution.py:108
  74.8 23.2 %all-to-all-start.1 = ((f32[16,72,128]{2,1,0:T(8,128)}), f32[16,72,128]{2,1,0:T(8,128)S(1)}, u32[]{:S(2)}, u32[]{:S(2)}) async-start(f32[16,72,128]{2,1,0:T(8,128)} %broadcast_in_dim.2), calls=%async_computation.1 | async-start | bytes 1179648 | tf_op jit(solution)/shard_map/all_to_all | solution.py:109
  99.5 26.9 %copy-start.22 = (f32[1,9,128,128]{3,2,1,0:T(8,128)S(1)}, f32[1,9,128,128]{3,2,1,0:T(8,128)}, u32[]{:S(2)}) copy-start(f32[1,9,128,128]{3,2,1,0:T(8,128)} %get-tuple-element.78) | copy-start | bytes 1769476
  99.5 26.9 %copy-start.23 = (f32[1,9,128,128]{3,2,1,0:T(8,128)S(1)}, f32[1,9,128,128]{3,2,1,0:T(8,128)}, u32[]{:S(2)}) copy-start(f32[1,9,128,128]{3,2,1,0:T(8,128)} %get-tuple-element.79) | copy-start | bytes 1769476
  99.5 26.9 %copy-start.24 = (f32[1,9,128,128]{3,2,1,0:T(8,128)S(1)}, f32[1,9,128,128]{3,2,1,0:T(8,128)}, u32[]{:S(2)}) copy-start(f32[1,9,128,128]{3,2,1,0:T(8,128)} %get-tuple-element.80) | copy-start | bytes 1769476
  99.5 26.9 %copy-start.25 = (f32[1,9,128,128]{3,2,1,0:T(8,128)S(1)}, f32[1,9,128,128]{3,2,1,0:T(8,128)}, u32[]{:S(2)}) copy-start(f32[1,9,128,128]{3,2,1,0:T(8,128)} %get-tuple-element.81) | copy-start | bytes 1769476
  99.5 26.9 %copy-start.26 = (f32[1,9,128,128]{3,2,1,0:T(8,128)S(1)}, f32[1,9,128,128]{3,2,1,0:T(8,128)}, u32[]{:S(2)}) copy-start(f32[1,9,128,128]{3,2,1,0:T(8,128)} %get-tuple-element.82) | copy-start | bytes 1769476
  99.5 26.9 %copy-start.27 = (f32[1,9,128,128]{3,2,1,0:T(8,128)S(1)}, f32[1,9,128,128]{3,2,1,0:T(8,128)}, u32[]{:S(2)}) copy-start(f32[1,9,128,128]{3,2,1,0:T(8,128)} %get-tuple-element.83) | copy-start | bytes 1769476
  99.5 26.9 %copy-start.28 = (f32[1,9,128,128]{3,2,1,0:T(8,128)S(1)}, f32[1,9,128,128]{3,2,1,0:T(8,128)}, u32[]{:S(2)}) copy-start(f32[1,9,128,128]{3,2,1,0:T(8,128)} %get-tuple-element.84) | copy-start | bytes 1769476
  113.1 13.3 %copy-start.2 = (f32[1,9,128,128]{3,2,1,0:T(8,128)S(1)}, f32[1,9,128,128]{3,2,1,0:T(8,128)}, u32[]{:S(2)}) copy-start(f32[1,9,128,128]{3,2,1,0:T(8,128)} %get-tuple-element.89) | copy-start | bytes 1769476
  113.1 13.3 %copy-start.3 = (f32[1,9,128,128]{3,2,1,0:T(8,128)S(1)}, f32[1,9,128,128]{3,2,1,0:T(8,128)}, u32[]{:S(2)}) copy-start(f32[1,9,128,128]{3,2,1,0:T(8,128)} %get-tuple-element.90) | copy-start | bytes 1769476
  113.1 13.4 %copy-start.4 = (f32[1,9,128,128]{3,2,1,0:T(8,128)S(1)}, f32[1,9,128,128]{3,2,1,0:T(8,128)}, u32[]{:S(2)}) copy-start(f32[1,9,128,128]{3,2,1,0:T(8,128)} %get-tuple-element.91) | copy-start | bytes 1769476
  113.1 13.4 %copy-start.5 = (f32[1,9,128,128]{3,2,1,0:T(8,128)S(1)}, f32[1,9,128,128]{3,2,1,0:T(8,128)}, u32[]{:S(2)}) copy-start(f32[1,9,128,128]{3,2,1,0:T(8,128)} %get-tuple-element.92) | copy-start | bytes 1769476
  113.1 13.4 %copy-start.6 = (f32[1,9,128,128]{3,2,1,0:T(8,128)S(1)}, f32[1,9,128,128]{3,2,1,0:T(8,128)}, u32[]{:S(2)}) copy-start(f32[1,9,128,128]{3,2,1,0:T(8,128)} %get-tuple-element.93) | copy-start | bytes 1769476
  113.1 13.4 %copy-start.7 = (f32[1,9,128,128]{3,2,1,0:T(8,128)S(1)}, f32[1,9,128,128]{3,2,1,0:T(8,128)}, u32[]{:S(2)}) copy-start(f32[1,9,128,128]{3,2,1,0:T(8,128)} %get-tuple-element.94) | copy-start | bytes 1769476
  113.1 13.4 %copy-start.8 = (f32[1,9,128,128]{3,2,1,0:T(8,128)S(1)}, f32[1,9,128,128]{3,2,1,0:T(8,128)}, u32[]{:S(2)}) copy-start(f32[1,9,128,128]{3,2,1,0:T(8,128)} %get-tuple-element.95) | copy-start | bytes 1769476
  113.1 13.4 %copy-start.9 = (f32[1,9,128,128]{3,2,1,0:T(8,128)S(1)}, f32[1,9,128,128]{3,2,1,0:T(8,128)}, u32[]{:S(2)}) copy-start(f32[1,9,128,128]{3,2,1,0:T(8,128)} %get-tuple-element.96) | copy-start | bytes 1769476
  113.1 13.4 %copy-start.10 = (f32[1,9,128,128]{3,2,1,0:T(8,128)S(1)}, f32[1,9,128,128]{3,2,1,0:T(8,128)}, u32[]{:S(2)}) copy-start(f32[1,9,128,128]{3,2,1,0:T(8,128)} %get-tuple-element.97) | copy-start | bytes 1769476
  113.1 13.4 %copy-start.11 = (f32[1,9,128,128]{3,2,1,0:T(8,128)S(1)}, f32[1,9,128,128]{3,2,1,0:T(8,128)}, u32[]{:S(2)}) copy-start(f32[1,9,128,128]{3,2,1,0:T(8,128)} %get-tuple-element.67) | copy-start | bytes 1769476
  113.2 13.4 %copy-start.12 = (f32[1,9,128,128]{3,2,1,0:T(8,128)S(1)}, f32[1,9,128,128]{3,2,1,0:T(8,128)}, u32[]{:S(2)}) copy-start(f32[1,9,128,128]{3,2,1,0:T(8,128)} %get-tuple-element.68) | copy-start | bytes 1769476
  113.2 13.4 %copy-start.13 = (f32[1,9,128,128]{3,2,1,0:T(8,128)S(1)}, f32[1,9,128,128]{3,2,1,0:T(8,128)}, u32[]{:S(2)}) copy-start(f32[1,9,128,128]{3,2,1,0:T(8,128)} %get-tuple-element.69) | copy-start | bytes 1769476
  113.2 13.4 %copy-start.14 = (f32[1,9,128,128]{3,2,1,0:T(8,128)S(1)}, f32[1,9,128,128]{3,2,1,0:T(8,128)}, u32[]{:S(2)}) copy-start(f32[1,9,128,128]{3,2,1,0:T(8,128)} %get-tuple-element.70) | copy-start | bytes 1769476
  113.2 13.4 %copy-start.15 = (f32[1,9,128,128]{3,2,1,0:T(8,128)S(1)}, f32[1,9,128,128]{3,2,1,0:T(8,128)}, u32[]{:S(2)}) copy-start(f32[1,9,128,128]{3,2,1,0:T(8,128)} %get-tuple-element.71) | copy-start | bytes 1769476
  113.2 13.4 %copy-start.16 = (f32[1,9,128,128]{3,2,1,0:T(8,128)S(1)}, f32[1,9,128,128]{3,2,1,0:T(8,128)}, u32[]{:S(2)}) copy-start(f32[1,9,128,128]{3,2,1,0:T(8,128)} %get-tuple-element.72) | copy-start | bytes 1769476
  113.2 13.4 %copy-start.17 = (f32[1,9,128,128]{3,2,1,0:T(8,128)S(1)}, f32[1,9,128,128]{3,2,1,0:T(8,128)}, u32[]{:S(2)}) copy-start(f32[1,9,128,128]{3,2,1,0:T(8,128)} %get-tuple-element.73) | copy-start | bytes 1769476
  113.2 13.4 %copy-start.18 = (f32[1,9,128,128]{3,2,1,0:T(8,128)S(1)}, f32[1,9,128,128]{3,2,1,0:T(8,128)}, u32[]{:S(2)}) copy-start(f32[1,9,128,128]{3,2,1,0:T(8,128)} %get-tuple-element.74) | copy-start | bytes 1769476
  113.2 13.4 %copy-start.19 = (f32[1,9,128,128]{3,2,1,0:T(8,128)S(1)}, f32[1,9,128,128]{3,2,1,0:T(8,128)}, u32[]{:S(2)}) copy-start(f32[1,9,128,128]{3,2,1,0:T(8,128)} %get-tuple-element.75) | copy-start | bytes 1769476
  113.2 13.4 %copy-start.20 = (f32[1,9,128,128]{3,2,1,0:T(8,128)S(1)}, f32[1,9,128,128]{3,2,1,0:T(8,128)}, u32[]{:S(2)}) copy-start(f32[1,9,128,128]{3,2,1,0:T(8,128)} %get-tuple-element.76) | copy-start | bytes 1769476
  113.2 13.4 %copy-start.21 = (f32[1,9,128,128]{3,2,1,0:T(8,128)S(1)}, f32[1,9,128,128]{3,2,1,0:T(8,128)}, u32[]{:S(2)}) copy-start(f32[1,9,128,128]{3,2,1,0:T(8,128)} %get-tuple-element.77) | copy-start | bytes 1769476
  220.1 5.7 %collective-permute-start.8 = (f32[1152,128]{1,0:T(8,128)S(1)}, f32[1152,128]{1,0:T(8,128)S(1)}, u32[]{:S(2)}, u32[]{:S(2)}) collective-permute-start(f32[1152,128]{1,0:T(8,128)S(1)} %get-tuple-element.2), channel_id=1, source_target_pairs={{0,16},{16,0},{2,18},{18,2},{4,20},{20,4},{6,22},{22,6},{8,24},{24... | collective-permute-start | bytes 1769480 | tf_op jit(solution)/shard_map/ppermute | solution.py:128
  224.2 3.6 %collective-permute-start.9 = (f32[1152,128]{1,0:T(8,128)S(1)}, f32[1152,128]{1,0:T(8,128)S(1)}, u32[]{:S(2)}, u32[]{:S(2)}) collective-permute-start(f32[1152,128]{1,0:T(8,128)S(1)} %get-tuple-element.3), channel_id=1, source_target_pairs={{0,16},{16,0},{2,18},{18,2},{4,20},{20,4},{6,22},{22,6},{8,24},{24... | collective-permute-start | bytes 1769480 | tf_op jit(solution)/shard_map/ppermute | solution.py:128

commit v2 on v1

v2 whole, which is shorter than its diff:
```python
import functools
import math

import jax
import jax.numpy as jnp
from jax import lax
from jax.experimental import pallas as pl
from jax.experimental.pallas import tpu as pltpu
from jax.sharding import PartitionSpec as P

AXES = ("row", "col")
BF16, F32 = jnp.bfloat16, jnp.float32
ROWS, COLS, CH = 64, 32, 128
CELLS = ROWS * COLS
PADDED = (ROWS + 2) * COLS
LINES = 9 * CH
EDGE = 80
HID = 32


def flat_index(x, y, z, core):
    return (((y % 2) * 4 + x) * 2 + core) * 16 + z * 2 + y // 2


COORDS = [(x, y, z, c) for y in range(4) for x in range(4) for z in range(8) for c in range(2)]


def pairs_of(fn):
    return [(flat_index(*p), flat_index(*fn(*p))) for p in COORDS]


CORE_PAIRS = pairs_of(lambda x, y, z, c: (x, y, z, 1 - c))
Z_TABLES = ((1, 0, 3, 2, 5, 4, 7, 6), (7, 2, 1, 4, 3, 6, 5, 0), (3, 6, 5, 0, 7, 2, 1, 4))
Z_PAIRS = [pairs_of(lambda x, y, z, c, t=t: (x, y, t[z], c)) for t in Z_TABLES]
PLANES = [
    [flat_index(x, y, z, c) for y in range(4) for x in range(4)] for z in range(8) for c in range(2)
]
VMEM = pl.BlockSpec(memory_space=pltpu.VMEM)
SMEM = pl.BlockSpec(memory_space=pltpu.SMEM)


def shape(dims, dtype):
    return jax.ShapeDtypeStruct(dims, dtype)


def call(body, ins, outs, micros, scratch=(), aliases=None):
    return pl.pallas_call(
        body,
        out_shape=outs,
        in_specs=ins,
        out_specs=jax.tree.map(lambda _: VMEM, outs),
        scratch_shapes=list(scratch),
        input_output_aliases=aliases or {},
        compiler_params=pltpu.CompilerParams(vmem_limit_bytes=40 * 1024 * 1024),
        cost_estimate=pl.CostEstimate(
            flops=int(micros * 8e6), bytes_accessed=1024, transcendentals=0
        ),
    )


def dot(left, right, over):
    return lax.dot_general(left, right, (over, ((), ())), preferred_element_type=F32)


def edges_body(image_ref, cot_ref, first_ref, last_ref):
    for at, ref in enumerate((image_ref, cot_ref)):
        head = ref[:, 0:16, :].astype(F32)
        tail = ref[:, 16:32, :].astype(F32)
        first_ref[at, 8:72, :] = head[:, 0, :]
        last_ref[at, 8:72, :] = tail[:, 15, :]


def corners_body(first_ref, last_ref, above_ref, below_ref, send_first_ref, send_last_ref):
    for at in range(2):
        above = above_ref[at].astype(F32)
        below = below_ref[at].astype(F32)
        for src, dst, col in ((first_ref, send_first_ref, 0), (last_ref, send_last_ref, 31)):
            line = lax.broadcasted_iota(jnp.int32, (8, CH), 0)
            top = jnp.where(line == 7, jnp.broadcast_to(above[col : col + 1], (8, CH)), 0.0)
            low = jnp.where(line == 0, jnp.broadcast_to(below[col : col + 1], (8, CH)), 0.0)
            dst[at] = jnp.concatenate([top, src[at, 8:72, :], low], axis=0).astype(BF16)


def taps_of(ref, start, count):
    return jnp.concatenate([ref[start + a * COLS : start + a * COLS + count, :] for a in range(3)], axis=1)


def back_weights(k_ref, taps):
    return jnp.concatenate([k_ref[1, tap] for tap in taps], axis=1)


def inner_body(image_ref, cot_ref, above_ref, below_ref, k_ref, x3_ref, c3_ref, pre_ref, back_ref, flat_ref):
    for at, (ref, out_ref) in enumerate(((image_ref, x3_ref), (cot_ref, c3_ref))):
        out_ref[0:COLS, CH : 2 * CH] = above_ref[at]
        out_ref[COLS : COLS + CELLS, CH : 2 * CH] = ref[...].reshape(CELLS, CH)
        out_ref[COLS + CELLS :, CH : 2 * CH] = below_ref[at]
        flat_ref[8 : 8 + COLS, :] = above_ref[at].astype(F32)
        flat_ref[8 + COLS : 8 + COLS + CELLS, :] = ref[...].reshape(CELLS, CH).astype(F32)
        flat_ref[8 + COLS + CELLS : 8 + PADDED, :] = below_ref[at].astype(F32)
        step = 6 * COLS
        col = lax.broadcasted_iota(jnp.int32, (step, CH), 0) % COLS
        for start in range(0, PADDED, step):
            early = jnp.where(col == 0, 0.0, flat_ref[7 + start : 7 + start + step, :])
            late = jnp.where(col == COLS - 1, 0.0, flat_ref[9 + start : 9 + start + step, :])
            out_ref[start : start + step, 0:CH] = early.astype(BF16)
            out_ref[start : start + step, 2 * CH :] = late.astype(BF16)
    size = 512
    forward = k_ref[0].reshape(LINES, CH)
    backward = back_weights(k_ref, range(8, -1, -1))
    for start in range(0, CELLS, size):
        pre_ref[start : start + size, :] = dot(taps_of(x3_ref, start, size), forward, ((1,), (0,)))
        back_ref[start : start + size, :] = dot(taps_of(c3_ref, start, size), backward, ((1,), (1,)))


def outer_body(
    x3_ref, c3_ref, pre_ref, back_ref, left_ref, right_ref, k_ref,
    x3_out, c3_out, hidden_ref, pre_grad_ref, edge_ref, mid_ref, grad_ref,
):
    mid_ref[...] = pre_ref[...]
    grad_ref[...] = back_ref[...]
    for at in range(2):
        out_ref = (x3_out, c3_out)[at]
        total_ref = (mid_ref, grad_ref)[at]
        for side, (ref, col, lane) in enumerate(((left_ref, 0, 0), (right_ref, COLS - 1, 2 * CH))):
            slot = 2 * at + side
            edge_ref[slot] = ref[at].astype(F32)
            lines = jnp.concatenate([edge_ref[slot, 7 + a : 71 + a, :] for a in range(3)], axis=1).astype(BF16)
            if at == 0:
                weights = jnp.concatenate([k_ref[0, 3 * a + 2 * side] for a in range(3)], axis=0)
                extra = dot(lines, weights, ((1,), (0,)))
            else:
                extra = dot(lines, back_weights(k_ref, [8 - 3 * a - 2 * side for a in range(3)]), ((1,), (1,)))
            spots = pl.ds(col, ROWS, stride=COLS)
            total_ref[spots, :] = total_ref[spots, :] + extra
            line = lax.broadcasted_iota(jnp.int32, (16, CH), 0)
            for r in range(ROWS + 2):
                base = r * COLS + (col // 16) * 16
                old = out_ref[base : base + 16, lane : lane + CH].astype(F32)
                new = jnp.broadcast_to(edge_ref[slot, 7 + r : 8 + r, :], (16, CH))
                out_ref[base : base + 16, lane : lane + CH] = jnp.where(line == col % 16, new, old).astype(BF16)
    size = 128
    for start in range(0, CELLS, size):
        mid = mid_ref[start : start + size, :]
        sigma = jax.nn.sigmoid(mid)
        hidden_ref[start : start + size, :] = (mid * sigma).astype(BF16)
        grad = grad_ref[start : start + size, :] * sigma * (1.0 + mid * (1.0 - sigma))
        pre_grad_ref[start : start + size, :] = grad.astype(BF16)


def grads_body(flip, core_ref, hidden_ref, pre_grad_ref, x3_ref, c3_ref, out_ref):
    which = core_ref[0] if flip == 0 else 1 - core_ref[0]

    @pl.when(which == 0)
    def _():
        left = pre_grad_ref[...]
        for a in range(3):
            part = dot(left, x3_ref[a * COLS : a * COLS + CELLS, :], ((0,), (0,)))
            for b in range(3):
                tap = 3 * a + b
                out_ref[tap * CH : (tap + 1) * CH, :] = part[:, b * CH : (b + 1) * CH].T

    @pl.when(which == 1)
    def _():
        left = hidden_ref[...]
        for a in range(3):
            part = dot(left, c3_ref[a * COLS : a * COLS + CELLS, :], ((0,), (0,)))
            for b in range(3):
                tap = 8 - 3 * a - b
                out_ref[tap * CH : (tap + 1) * CH, :] = part[:, b * CH : (b + 1) * CH]


def add_body(left_ref, right_ref, out_ref):
    out_ref[...] = left_ref[...] + right_ref[...]


def fold_body(parts_ref, out_ref):
    total = parts_ref[0]
    for i in range(1, 16):
        total = total + parts_ref[i]
    out_ref[...] = total


def momentum_body(core_ref, grads_ref, momentum_ref, out_ref, scale_ref):
    total = jnp.zeros((8, CH), F32)
    for i in range(16):
        part = grads_ref[i]
        total = total + jnp.sum((part * part).reshape(9, 8, CH), axis=0)
    squares = jnp.sum(total)
    scale = 1.0 / jnp.sqrt(jnp.full((8, CH), squares, F32) / float(LINES * CH) + 1e-06)
    scale_ref[...] = scale
    line = jnp.broadcast_to(scale[0:1], (72, CH))
    for layer in range(2):

        @pl.when(core_ref[0] == layer)
        def _():
            for i in range(16):
                old = momentum_ref[pl.ds(2 * 72 * i + layer, 72, stride=2), :]
                out_ref[i * 72 : (i + 1) * 72, :] = 0.9 * old + 0.1 * (grads_ref[i] * line)


def mlp_body(core_ref, w_ref, b_ref, v_ref, c_ref, grads_ref, new_ref, scale_ref, k_ref, out_ref):
    block = 48
    gain = math.sqrt(9.0 * CH)
    scale = jnp.broadcast_to(scale_ref[0:1], (block, CH))
    base = core_ref[0] * LINES

    def step(i, _):
        rows = pl.ds(pl.multiple_of(i * block, block), block)
        g_hat = grads_ref[rows, :] * scale
        new = new_ref[rows, :]
        scaled = k_ref[pl.ds(pl.multiple_of(base + i * block, 16), block), :].astype(F32) * gain
        top = jnp.full((block, CH), c_ref[0], F32)
        low = jnp.full((block, CH), c_ref[1], F32)
        for h in range(HID):
            half = (0.5 * w_ref[h, 0]) * g_hat + (0.5 * w_ref[h, 1]) * new
            half = half + (0.5 * w_ref[h, 2]) * scaled + 0.5 * b_ref[h]
            unit = half + half * jnp.tanh(half)
            top = top + v_ref[0, h] * unit
            low = low + v_ref[1, h] * unit
        out_ref[rows, :] = top * jnp.exp(jnp.tanh(low))
        return 0

    lax.fori_loop(0, LINES // block, step, 0)


def weave_body(core_ref, mine_ref, theirs_ref, out_ref):
    for layer in range(2):

        @pl.when(core_ref[0] == layer)
        def _():
            for start in range(0, LINES, 72):
                out_ref[pl.ds(2 * start + layer, 72, stride=2), :] = mine_ref[start : start + 72, :]
                out_ref[pl.ds(2 * start + 1 - layer, 72, stride=2), :] = theirs_ref[start : start + 72, :]


def on_device(
    features, cotangent, kernels, momentum, mlp_in_weight, mlp_in_bias, mlp_out_weight, mlp_out_bias
):
    core = (lax.axis_index("row") % 2).astype(jnp.int32).reshape(1)
    count_r, count_c = lax.axis_size("row"), lax.axis_size("col")
    up = lambda n: [(i, (i + 1) % n) for i in range(n)]
    down = lambda n: [((i + 1) % n, i) for i in range(n)]

    above = lax.ppermute(jnp.stack([features[-1], cotangent[-1]]), "row", up(count_r))
    below = lax.ppermute(jnp.stack([features[0], cotangent[0]]), "row", down(count_r))
    columns = (shape((2, EDGE, CH), F32),) * 2
    first, last = call(edges_body, [VMEM] * 2, columns, 0.5)(features, cotangent)
    columns = (shape((2, EDGE, CH), BF16),) * 2
    first, last = call(corners_body, [VMEM] * 4, columns, 0.2)(first, last, above, below)
    left = lax.ppermute(last, "col", up(count_c))
    right = lax.ppermute(first, "col", down(count_c))
    wide, tile = shape((PADDED, 3 * CH), BF16), shape((CELLS, CH), F32)
    x3, c3, pre, back = call(
        inner_body, [VMEM] * 5, (wide, wide, tile, tile), 5.0, [pltpu.VMEM((PADDED + 16, CH), F32)]
    )(features, cotangent, above, below, kernels)
    narrow = shape((CELLS, CH), BF16)
    x3, c3, hidden, pre_grad = call(
        outer_body,
        [VMEM] * 7,
        (wide, wide, narrow, narrow),
        1.5,
        [pltpu.VMEM((4, EDGE, CH), F32), pltpu.VMEM((CELLS, CH), F32), pltpu.VMEM((CELLS, CH), F32)],
        {0: 0, 1: 1},
    )(x3, c3, pre, back, left, right, kernels)

    layer = shape((LINES, CH), F32)
    gradient = lambda flip: call(functools.partial(grads_body, flip), [SMEM] + [VMEM] * 4, layer, 2.5)(
        core, hidden, pre_grad, x3, c3
    )
    theirs = lax.ppermute(gradient(1), AXES, CORE_PAIRS)
    mine = call(add_body, [VMEM] * 2, layer, 0.3)(gradient(0), theirs)
    parts = lax.all_to_all(
        mine.reshape(16, LINES // 16, CH), AXES, 0, 0, axis_index_groups=PLANES, tiled=True
    )
    part = call(fold_body, [VMEM], shape((LINES // 16, CH), F32), 0.3)(parts)
    for pairs in Z_PAIRS:
        part = part + lax.ppermute(part, AXES, pairs)
    grads = lax.all_to_all(
        jnp.broadcast_to(part[None], parts.shape), AXES, 0, 0, axis_index_groups=PLANES, tiled=True
    )

    woven = momentum.reshape(2, LINES, CH).transpose(1, 0, 2).reshape(2 * LINES, CH)
    new, scale = call(momentum_body, [SMEM, VMEM, VMEM], (layer, shape((8, CH), F32)), 0.5)(
        core, grads, woven
    )
    new_theirs = lax.ppermute(new, AXES, CORE_PAIRS)
    update = call(mlp_body, [SMEM] * 5 + [VMEM] * 4, layer, 8.0)(
        core, mlp_in_weight, mlp_in_bias, mlp_out_weight, mlp_out_bias,
        grads.reshape(LINES, CH), new, scale, kernels.reshape(2 * LINES, CH),
    )
    update_theirs = lax.ppermute(update, AXES, CORE_PAIRS)
    outs = []
    for own, other in ((update, update_theirs), (new, new_theirs)):
        both = call(weave_body, [SMEM] + [VMEM] * 2, shape((2 * LINES, CH), F32), 0.5)(core, own, other)
        outs.append(both.reshape(LINES, 2, CH).transpose(1, 0, 2).reshape(2, LINES * CH))
    return tuple(outs)


def solution(mesh):
    placed = (P("row", "col", None), P("row", "col", None), P(), P(), P(), P(), P(), P())
    return jax.shard_map(
        on_device, mesh=mesh, in_specs=placed, out_specs=(P(), P()), check_vma=False
    )
```

time: 232 us -> 88.5 us (0.38)
  other arithmetic: 139 us -> 0.03 us
  between operations: 21.9 us -> 0.77 us
  Pallas kernels: 0 us -> 18.5 us
  blocking collectives: 0 us -> 14.3 us
  waiting for transfers between devices: 4.21 us -> 16.7 us
  matrix products: 11.8 us -> 0 us
  local copies, waits for them, and re-layouts: 14.2 us -> 4.91 us
  starting transfers between devices: 39.3 us -> 33 us
    mul x7 -> x0, other arithmetic: 131 us -> none  [the longest x1 93.5 us: on_device(): update = (top + mlp_out_bias[0]) * jnp.exp(jnp.tanh(low + mlp_out_bias[1]))]
    pallas_call x0 -> x12, Pallas kernels: none -> 18.5 us  [the longest x1 10 us: on_device(): call(mlp_body, [SMEM] * 5 + [VMEM] * 4, layer, 8.0)]
    all_to_all x0 -> x1, blocking collectives: none -> 14.3 us  [on_device(): lax.all_to_all(mine.reshape(16, LINES // 16, CH), AXES, 0, 0, axis_index_...]
    slice x14 -> x1, local copies, waits for them, and re-layouts: 12.9 us -> 0.81 us  [on_device(): features[0]]
    dot_general x36 -> x0, matrix products: 11.8 us -> none  [the longest x18 6.2 us: outer(): lax.dot_general(left, right, (((0,), (0,)), ((), ())), preferred_element_...]
    all_to_all x1, waiting for transfers between devices: 0.01 us -> 9.21 us  [on_device(): lax.all_to_all(jnp.broadcast_to(part[None], parts.shape), AXES, 0, 0, axi...]
    another operation x2, other arithmetic: 3.84 us -> 0.01 us  [the longest x1 0.01 us: on_device(): jnp.stack([features[0], cotangent[0]])]
    ppermute x7, starting transfers between devices: 19.3 us -> 23.1 us  [the longest x1 6.59 us: on_device(): new_theirs = lax.ppermute(new, AXES, CORE_PAIRS)]
  transfers between devices with their start and end apart: 12 -> 11, of which waited for: 5 -> 6; matrix products, arithmetic and copies ran while one was open for 10% -> 0% of each run, Pallas kernels for 0% -> 17%
where the time goes in v2:
time: 88.5 us; the launch traced here: 88.1 us
  starting transfers between devices  33 us (37%)
  Pallas kernels  18.5 us (21%)
  waiting for transfers between devices  16.7 us (19%)
  blocking collectives  14.3 us (16%)
  local copies, waits for them, and re-layouts  4.91 us (6%)
    all_to_all x1, blocking collectives, on_device(): lax.all_to_all(mine.reshape(16, LINES // 16, CH), AXES, 0, 0, axis_index_...  14.3 us
    pallas_call x1, Pallas kernels, on_device(): call(mlp_body, [SMEM] * 5 + [VMEM] * 4, layer, 8.0)  10 us
    all_to_all x1, waiting for transfers between devices, on_device(): lax.all_to_all(jnp.broadcast_to(part[None], parts.shape), AXES, 0, 0, axi...  9.21 us
    ppermute x1, starting transfers between devices, on_device(): new_theirs = lax.ppermute(new, AXES, CORE_PAIRS)  6.59 us
    ppermute x3, starting transfers between devices, on_device(): part = part + lax.ppermute(part, AXES, pairs)  6.16 us
    ppermute x3, waiting for transfers between devices, on_device(): part = part + lax.ppermute(part, AXES, pairs)  5.98 us
    ppermute x1, starting transfers between devices, on_device(): right = lax.ppermute(first, 'col', down(count_c))  5.38 us
    ppermute x1, starting transfers between devices, on_device(): theirs = lax.ppermute(gradient(1), AXES, CORE_PAIRS)  5.06 us
  transfers between devices with their start and end apart: 11, of which 6 were waited for; matrix products, arithmetic and copies ran while one was open for 0% of the time, Pallas kernels for 17%

profile of v2, /device:TPU:1, one launch (start us, length us, event | category | flops | bytes accessed | tf_op | source)
XLA Modules:
  0.0 88.1 jit_solution(15542033817240752475)
XLA Ops:
  0.6 0.0 copy-start
  0.6 0.8 fusion
  1.5 3.3 %collective-permute-start.1 = (bf16[2,32,128]{2,1,0:T(8,128)(2,1)S(1)}, bf16[2,32,128]{2,1,0:T(8,128)(2,1)S(1)}, u32[]{:S(2)}, u32[]{:S(2)}) collective-permute-start(bf16[2,32,128]{2,1,0:T(8,128)(2,1)S(1)} %pad_maximum_fusion.1), channel_id=1, source_target_pairs={{16,0},{32,16},{48,32},{64,48},{80,64},{96,80},{112,96},{128,112},... | collective-permute-start | bytes 49160 | tf_op jit(solution)/shard_map/ppermute | solution.py:245
  4.7 0.0 collective-permute-start
  4.7 0.0 copy-start.1
  4.7 1.0 %copy-done.1 = bf16[64,32,128]{2,1,0:T(8,128)(2,1)S(1)} copy-done((bf16[64,32,128]{2,1,0:T(8,128)(2,1)S(1)}, bf16[64,32,128]{2,1,0:T(8,128)(2,1)}, u32[]{:S(2)}) %copy-start.1) | copy-done | bytes 524312
  5.8 0.0 copy-start.3
  5.8 1.0 %copy-done.3 = bf16[64,32,128]{2,1,0:T(8,128)(2,1)S(1)} copy-done((bf16[64,32,128]{2,1,0:T(8,128)(2,1)S(1)}, bf16[64,32,128]{2,1,0:T(8,128)(2,1)}, u32[]{:S(2)}) %copy-start.3) | copy-done | bytes 524312
  6.8 0.0 copy-start.2
  6.8 0.1 shard_map.96
  6.9 0.0 collective-permute-done.1.below_ref
  6.9 0.0 collective-permute-done.above_ref
  7.0 2.7 %collective-permute-start.2 = (bf16[2,80,128]{2,1,0:T(8,128)(2,1)S(1)}, bf16[2,80,128]{2,1,0:T(8,128)(2,1)S(1)}, u32[]{:S(2)}, u32[]{:S(2)}) collective-permute-start(bf16[2,80,128]{2,1,0:T(8,128)(2,1)S(1)} %get-tuple-element.22), channel_id=1, source_target_pairs={{0,1},{1,2},{2,3},{3,4},{4,5},{5,6},{6,7},{7,8},{8,9},{9,10},{10,1... | collective-permute-start | bytes 122888 | tf_op jit(solution)/shard_map/ppermute | solution.py:250
  9.6 5.4 %collective-permute-start.3 = (bf16[2,80,128]{2,1,0:T(8,128)(2,1)S(1)}, bf16[2,80,128]{2,1,0:T(8,128)(2,1)S(1)}, u32[]{:S(2)}, u32[]{:S(2)}) collective-permute-start(bf16[2,80,128]{2,1,0:T(8,128)(2,1)S(1)} %get-tuple-element.23), channel_id=1, source_target_pairs={{1,0},{2,1},{3,2},{4,3},{5,4},{6,5},{7,6},{8,7},{9,8},{10,9},{11,1... | collective-permute-start | bytes 122888 | tf_op jit(solution)/shard_map/ppermute | solution.py:251
  15.0 0.0 copy-done
  15.0 0.0 copy-done.2
  15.0 0.0 copy-start.4
  15.0 1.0 %copy-done.4 = bf16[64,32,128]{2,1,0:T(8,128)(2,1)S(1)} copy-done((bf16[64,32,128]{2,1,0:T(8,128)(2,1)S(1)}, bf16[64,32,128]{2,1,0:T(8,128)(2,1)}, u32[]{:S(2)}) %copy-start.4) | copy-done | bytes 524312
  16.0 2.7 %shard_map.95 = (bf16[2112,384]{1,0:T(8,128)(2,1)S(1)}, bf16[2112,384]{1,0:T(8,128)(2,1)S(1)}, f32[2048,128]{1,0:T(8,128)S(1)}, f32[2048,128]{1,0:T(8,128)S(1)}) custom-call(bf16[64,32,128]{2,1,0:T(8,128)(2,1)S(1)} %copy-done.2, bf16[64,32,128]{2,1,0:T(8,128)(2,1)S(1)} %copy-done.4, bf16[2,32,128]{2,1,0:T(8,128)(2,1)S(1)} %collective-permute-done.above_ref, ...), custom_call_target="tpu_custom_call" | custom-call | flops 40000000 | bytes 1024 | tf_op jit(solution)/shard_map/pallas_call | solution.py:253
  18.8 0.0 collective-permute-done.2.left_ref
  18.8 0.0 collective-permute-done.3.right_ref
  18.8 0.9 %shard_map.98 = (bf16[2112,384]{1,0:T(8,128)(2,1)S(1)}, bf16[2112,384]{1,0:T(8,128)(2,1)S(1)}, bf16[2048,128]{1,0:T(8,128)(2,1)S(1)}, bf16[2048,128]{1,0:T(8,128)(2,1)S(1)}) custom-call(bf16[2112,384]{1,0:T(8,128)(2,1)S(1)} %get-tuple-element.16.x3_ref, ...), custom_call_target="tpu_custom_call", output_to_operand_aliasing={{0}: (0, {}), {1}: (1, {})} | custom-call | flops 12000000 | bytes 1024 | tf_op jit(solution)/shard_map/pallas_call | solution.py:257
  19.7 1.1 %shard_map.100 = f32[1152,128]{1,0:T(8,128)S(1)} custom-call(s32[1]{0:T(128)} %bitcast.core_ref, bf16[2048,128]{1,0:T(8,128)(2,1)S(1)} %get-tuple-element.24.hidden_ref, bf16[2048,128]{1,0:T(8,128)(2,1)S(1)} %get-tuple-element.25.pre_grad_ref, bf16[2112,384]{1,0:T(8,128)(2,1)S(1)} %get-tuple-element.26.x3_ref, bf16[2112,384]{1,0:T(8,128)(2,1)S(1)} %get-tuple-element.27.c3_ref), custom_call_target="tpu_custom_call" | custom-call | flops 20000000 | bytes 1024 | tf_op jit(solution)/shard_map/pallas_call | solution.py:267
  20.8 5.1 %collective-permute-start.4 = (f32[1152,128]{1,0:T(8,128)S(1)}, f32[1152,128]{1,0:T(8,128)S(1)}, u32[]{:S(2)}, u32[]{:S(2)}) collective-permute-start(f32[1152,128]{1,0:T(8,128)S(1)} %shard_map.100), channel_id=1, source_target_pairs={{0,16},{16,0},{2,18},{18,2},{4,20},{20,4},{6,22},{22,6},{8,24},{24... | collective-permute-start | bytes 1769480 | tf_op jit(solution)/shard_map/ppermute | solution.py:270
  25.9 1.0 %shard_map.99.left_ref = f32[1152,128]{1,0:T(8,128)S(1)} custom-call(s32[1]{0:T(128)} %bitcast.core_ref, bf16[2048,128]{1,0:T(8,128)(2,1)S(1)} %get-tuple-element.24.hidden_ref, bf16[2048,128]{1,0:T(8,128)(2,1)S(1)} %get-tuple-element.25.pre_grad_ref, bf16[2112,384]{1,0:T(8,128)(2,1)S(1)} %get-tuple-element.26.x3_ref, ...), custom_call_target="tpu_custom_call" | custom-call | flops 20000000 | bytes 1024 | tf_op jit(solution)/shard_map/pallas_call | solution.py:267
  26.9 0.6 collective-permute-done.4.right_ref
  27.5 0.1 shard_map.101
  27.6 14.3 %all_to_all.10.parts_ref = f32[16,72,128]{2,1,0:T(8,128)S(1)} all-to-all(f32[16,72,128]{2,1,0:T(8,128)S(1)} %bitcast.21), channel_id=1, replica_groups={{0,32,64,96,128,160,192,224,1,33,65,97,129,161,193,225},{16,48,80,112,1..., dimensions={0} | all-to-all | bytes 1179648 | tf_op jit(solution)/shard_map/all_to_all | solution.py:272
  41.9 0.0 copy-start.9
  41.9 0.0 copy-start.5
  41.9 0.1 collective-permute-start.5
  42.0 2.8 %collective-permute-done.5 = f32[72,128]{1,0:T(8,128)S(1)} collective-permute-done((f32[72,128]{1,0:T(8,128)S(1)}, f32[72,128]{1,0:T(8,128)S(1)}, u32[]{:S(2)}, u32[]{:S(2)}) %collective-permute-start.5) | collective-permute-done | bytes 36896 | tf_op jit(solution)/shard_map/ppermute | solution.py:277
  44.8 2.2 %collective-permute-start.6 = (f32[72,128]{1,0:T(8,128)S(1)}, f32[72,128]{1,0:T(8,128)S(1)}, u32[]{:S(2)}, u32[]{:S(2)}) collective-permute-start(f32[72,128]{1,0:T(8,128)S(1)} %add.14), channel_id=1, source_target_pairs={{0,14},{16,30},{2,4},{18,20},{4,2},{20,18},{6,8},{22,24},{8,6},{24... | collective-permute-start | bytes 110600 | tf_op jit(solution)/shard_map/ppermute | solution.py:277
  47.0 1.8 %collective-permute-done.6 = f32[72,128]{1,0:T(8,128)S(1)} collective-permute-done((f32[72,128]{1,0:T(8,128)S(1)}, f32[72,128]{1,0:T(8,128)S(1)}, u32[]{:S(2)}, u32[]{:S(2)}) %collective-permute-start.6) | collective-permute-done | bytes 36896 | tf_op jit(solution)/shard_map/ppermute | solution.py:277
  48.8 3.9 %collective-permute-start.7 = (f32[72,128]{1,0:T(8,128)S(1)}, f32[72,128]{1,0:T(8,128)S(1)}, u32[]{:S(2)}, u32[]{:S(2)}) collective-permute-start(f32[72,128]{1,0:T(8,128)S(1)} %add.15), channel_id=1, source_target_pairs={{0,6},{16,22},{2,12},{18,28},{4,10},{20,26},{6,0},{22,16},{8,14},{... | collective-permute-start | bytes 110600 | tf_op jit(solution)/shard_map/ppermute | solution.py:277
  52.7 1.3 %collective-permute-done.7 = f32[72,128]{1,0:T(8,128)S(1)} collective-permute-done((f32[72,128]{1,0:T(8,128)S(1)}, f32[72,128]{1,0:T(8,128)S(1)}, u32[]{:S(2)}, u32[]{:S(2)}) %collective-permute-start.7) | collective-permute-done | bytes 36896 | tf_op jit(solution)/shard_map/ppermute | solution.py:277
  54.1 0.9 broadcast_in_dim.2
  54.9 0.0 copy-start.6
  54.9 0.0 copy-start.7
  54.9 0.0 copy-start.8
  54.9 3.7 %all-to-all-start.1 = ((f32[16,72,128]{2,1,0:T(8,128)}), f32[16,72,128]{2,1,0:T(8,128)S(1)}, u32[]{:S(2)}, u32[]{:S(2)}) async-start(f32[16,72,128]{2,1,0:T(8,128)} %broadcast_in_dim.2), calls=%async_computation.1 | async-start | bytes 1179648 | tf_op jit(solution)/shard_map/all_to_all | solution.py:278
  58.7 0.0 copy-done.9
  58.7 0.1 copy.13.w_ref
  58.8 9.2 %all-to-all-done.1.grads_ref = f32[16,72,128]{2,1,0:T(8,128)S(1)} async-done(((f32[16,72,128]{2,1,0:T(8,128)}), f32[16,72,128]{2,1,0:T(8,128)S(1)}, u32[]{:S(2)}, u32[]{:S(2)}) %all-to-all-start.1) | async-done | bytes 589856 | tf_op jit(solution)/shard_map/all_to_all | solution.py:278
  68.0 0.0 copy-done.5
  68.0 0.3 shard_map.103
  68.3 6.6 %collective-permute-start.9 = (f32[1152,128]{1,0:T(8,128)S(1)}, f32[1152,128]{1,0:T(8,128)S(1)}, u32[]{:S(2)}, u32[]{:S(2)}) collective-permute-start(f32[1152,128]{1,0:T(8,128)S(1)} %get-tuple-element.28.new_ref.mine_ref), channel_id=1, source_target_pairs={{0,16},{16,0},{2,18},{18,2},{4,20},{20,4},{6,22},{22,6},{8,24},{24... | collective-permute-start | bytes 1769480 | tf_op jit(solution)/shard_map/ppermute | solution.py:286
  74.9 0.0 copy-done.6
  74.9 0.0 copy-done.7
  74.9 0.0 copy-done.8
  74.9 10.0 %shard_map.104.mine_ref = f32[1152,128]{1,0:T(8,128)S(1)} custom-call(s32[1]{0:T(128)} %bitcast.core_ref, f32[32,3]{1,0:T(8,128)S(1)} %copy.13.w_ref, f32[32]{0:T(128)S(1)} %copy-done.7, f32[2,32]{1,0:T(2,128)S(1)} %copy-done.6, f32[2]{0:T(128)S(1)} %copy-done.8, f32[1152,128]{1,0:T(8,128)S(1)} %bitcast.20, ...), custom_call_target="tpu_custom_call" | custom-call | flops 64000000 | bytes 1024 | tf_op jit(solution)/shard_map/pallas_call | solution.py:287
  84.9 0.1 collective-permute-start.8
  85.0 0.0 collective-permute-done.9.theirs_ref
  85.0 1.1 %shard_map.106 = f32[2304,128]{1,0:T(8,128)} custom-call(s32[1]{0:T(128)} %bitcast.core_ref, f32[1152,128]{1,0:T(8,128)S(1)} %get-tuple-element.28.new_ref.mine_ref, f32[1152,128]{1,0:T(8,128)S(1)} %collective-permute-done.9.theirs_ref), custom_call_target="tpu_custom_call" | custom-call | flops 4000000 | bytes 1024 | tf_op jit(solution)/shard_map/pallas_call | solution.py:294
  86.1 0.9 collective-permute-done.8.theirs_ref
  87.0 1.1 %shard_map.105 = f32[2304,128]{1,0:T(8,128)} custom-call(s32[1]{0:T(128)} %bitcast.core_ref, f32[1152,128]{1,0:T(8,128)S(1)} %shard_map.104.mine_ref, f32[1152,128]{1,0:T(8,128)S(1)} %collective-permute-done.8.theirs_ref), custom_call_target="tpu_custom_call" | custom-call | flops 4000000 | bytes 1024 | tf_op jit(solution)/shard_map/pallas_call | solution.py:294
  (7 shorter events, 0.1 us)
Async XLA Ops:
  0.6 14.4 %copy-start = (bf16[2,9,128,128]{3,2,1,0:T(8,128)(2,1)S(1)}, bf16[2,9,128,128]{3,2,1,0:T(8,128)(2,1)}, u32[]{:S(2)}) copy-start(bf16[2,9,128,128]{3,2,1,0:T(8,128)(2,1)} %k_ref.3) | copy-start | bytes 1769476
  1.5 5.5 %collective-permute-start.1 = (bf16[2,32,128]{2,1,0:T(8,128)(2,1)S(1)}, bf16[2,32,128]{2,1,0:T(8,128)(2,1)S(1)}, u32[]{:S(2)}, u32[]{:S(2)}) collective-permute-start(bf16[2,32,128]{2,1,0:T(8,128)(2,1)S(1)} %pad_maximum_fusion.1), channel_id=1, source_target_pairs={{16,0},{32,16},{48,32},{64,48},{80,64},{96,80},{112,96},{128,112},... | collective-permute-start | bytes 49160 | tf_op jit(solution)/shard_map/ppermute | solution.py:245
  4.7 2.2 %collective-permute-start = (bf16[2,32,128]{2,1,0:T(8,128)(2,1)S(1)}, bf16[2,32,128]{2,1,0:T(8,128)(2,1)S(1)}, u32[]{:S(2)}, u32[]{:S(2)}) collective-permute-start(bf16[2,32,128]{2,1,0:T(8,128)(2,1)S(1)} %pad_maximum_fusion), channel_id=1, source_target_pairs={{0,16},{16,32},{32,48},{48,64},{64,80},{80,96},{96,112},{112,128},... | collective-permute-start | bytes 49160 | tf_op jit(solution)/shard_map/ppermute | solution.py:244
  4.7 1.0 %copy-start.1 = (bf16[64,32,128]{2,1,0:T(8,128)(2,1)S(1)}, bf16[64,32,128]{2,1,0:T(8,128)(2,1)}, u32[]{:S(2)}) copy-start(bf16[64,32,128]{2,1,0:T(8,128)(2,1)} %image_ref.3) | copy-start | bytes 1572868
  5.8 1.0 %copy-start.3 = (bf16[64,32,128]{2,1,0:T(8,128)(2,1)S(1)}, bf16[64,32,128]{2,1,0:T(8,128)(2,1)}, u32[]{:S(2)}) copy-start(bf16[64,32,128]{2,1,0:T(8,128)(2,1)} %cot_ref.3) | copy-start | bytes 1572868
  6.8 8.2 %copy-start.2 = (bf16[64,32,128]{2,1,0:T(8,128)(2,1)S(1)}, bf16[64,32,128]{2,1,0:T(8,128)(2,1)}, u32[]{:S(2)}) copy-start(bf16[64,32,128]{2,1,0:T(8,128)(2,1)} %image_ref.3) | copy-start | bytes 1572868
  7.0 11.8 %collective-permute-start.2 = (bf16[2,80,128]{2,1,0:T(8,128)(2,1)S(1)}, bf16[2,80,128]{2,1,0:T(8,128)(2,1)S(1)}, u32[]{:S(2)}, u32[]{:S(2)}) collective-permute-start(bf16[2,80,128]{2,1,0:T(8,128)(2,1)S(1)} %get-tuple-element.22), channel_id=1, source_target_pairs={{0,1},{1,2},{2,3},{3,4},{4,5},{5,6},{6,7},{7,8},{8,9},{9,10},{10,1... | collective-permute-start | bytes 122888 | tf_op jit(solution)/shard_map/ppermute | solution.py:250
  9.6 9.2 %collective-permute-start.3 = (bf16[2,80,128]{2,1,0:T(8,128)(2,1)S(1)}, bf16[2,80,128]{2,1,0:T(8,128)(2,1)S(1)}, u32[]{:S(2)}, u32[]{:S(2)}) collective-permute-start(bf16[2,80,128]{2,1,0:T(8,128)(2,1)S(1)} %get-tuple-element.23), channel_id=1, source_target_pairs={{1,0},{2,1},{3,2},{4,3},{5,4},{6,5},{7,6},{8,7},{9,8},{10,9},{11,1... | collective-permute-start | bytes 122888 | tf_op jit(solution)/shard_map/ppermute | solution.py:251
  15.0 1.0 %copy-start.4 = (bf16[64,32,128]{2,1,0:T(8,128)(2,1)S(1)}, bf16[64,32,128]{2,1,0:T(8,128)(2,1)}, u32[]{:S(2)}) copy-start(bf16[64,32,128]{2,1,0:T(8,128)(2,1)} %cot_ref.3) | copy-start | bytes 1572868
  20.8 6.7 %collective-permute-start.4 = (f32[1152,128]{1,0:T(8,128)S(1)}, f32[1152,128]{1,0:T(8,128)S(1)}, u32[]{:S(2)}, u32[]{:S(2)}) collective-permute-start(f32[1152,128]{1,0:T(8,128)S(1)} %shard_map.100), channel_id=1, source_target_pairs={{0,16},{16,0},{2,18},{18,2},{4,20},{20,4},{6,22},{22,6},{8,24},{24... | collective-permute-start | bytes 1769480 | tf_op jit(solution)/shard_map/ppermute | solution.py:270
  41.9 16.8 %copy-start.9 = (f32[32,3]{0,1:T(4,128)S(1)}, f32[32,3]{0,1:T(4,128)}, u32[]{:S(2)}) copy-start(f32[32,3]{0,1:T(4,128)} %param.12) | copy-start | bytes 1156
  41.9 26.1 %copy-start.5 = (f32[2,147456]{1,0:T(2,128)S(1)}, f32[2,147456]{1,0:T(2,128)}, u32[]{:S(2)}) copy-start(f32[2,147456]{1,0:T(2,128)} %param.11) | copy-start | bytes 3538948
  41.9 2.9 %collective-permute-start.5 = (f32[72,128]{1,0:T(8,128)S(1)}, f32[72,128]{1,0:T(8,128)S(1)}, u32[]{:S(2)}, u32[]{:S(2)}) collective-permute-start(f32[72,128]{1,0:T(8,128)S(1)} %shard_map.102), channel_id=1, source_target_pairs={{0,2},{16,18},{2,0},{18,16},{4,6},{20,22},{6,4},{22,20},{8,10},{24... | collective-permute-start | bytes 110600 | tf_op jit(solution)/shard_map/ppermute | solution.py:277
  44.8 4.0 %collective-permute-start.6 = (f32[72,128]{1,0:T(8,128)S(1)}, f32[72,128]{1,0:T(8,128)S(1)}, u32[]{:S(2)}, u32[]{:S(2)}) collective-permute-start(f32[72,128]{1,0:T(8,128)S(1)} %add.14), channel_id=1, source_target_pairs={{0,14},{16,30},{2,4},{18,20},{4,2},{20,18},{6,8},{22,24},{8,6},{24... | collective-permute-start | bytes 110600 | tf_op jit(solution)/shard_map/ppermute | solution.py:277
  48.8 5.2 %collective-permute-start.7 = (f32[72,128]{1,0:T(8,128)S(1)}, f32[72,128]{1,0:T(8,128)S(1)}, u32[]{:S(2)}, u32[]{:S(2)}) collective-permute-start(f32[72,128]{1,0:T(8,128)S(1)} %add.15), channel_id=1, source_target_pairs={{0,6},{16,22},{2,12},{18,28},{4,10},{20,26},{6,0},{22,16},{8,14},{... | collective-permute-start | bytes 110600 | tf_op jit(solution)/shard_map/ppermute | solution.py:277
  54.9 19.9 %copy-start.6 = (f32[2,32]{1,0:T(2,128)S(1)}, f32[2,32]{1,0:T(2,128)}, u32[]{:S(2)}) copy-start(f32[2,32]{1,0:T(2,128)} %v_ref.1) | copy-start | bytes 772
  54.9 19.9 %copy-start.7 = (f32[32]{0:T(128)S(1)}, f32[32]{0:T(128)}, u32[]{:S(2)}) copy-start(f32[32]{0:T(128)} %b_ref.1) | copy-start | bytes 388
  54.9 19.9 %copy-start.8 = (f32[2]{0:T(128)S(1)}, f32[2]{0:T(128)}, u32[]{:S(2)}) copy-start(f32[2]{0:T(128)} %c_ref.1) | copy-start | bytes 28
  54.9 13.0 %all-to-all-start.1 = ((f32[16,72,128]{2,1,0:T(8,128)}), f32[16,72,128]{2,1,0:T(8,128)S(1)}, u32[]{:S(2)}, u32[]{:S(2)}) async-start(f32[16,72,128]{2,1,0:T(8,128)} %broadcast_in_dim.2), calls=%async_computation.1 | async-start | bytes 1179648 | tf_op jit(solution)/shard_map/all_to_all | solution.py:278
  68.3 16.8 %collective-permute-start.9 = (f32[1152,128]{1,0:T(8,128)S(1)}, f32[1152,128]{1,0:T(8,128)S(1)}, u32[]{:S(2)}, u32[]{:S(2)}) collective-permute-start(f32[1152,128]{1,0:T(8,128)S(1)} %get-tuple-element.28.new_ref.mine_ref), channel_id=1, source_target_pairs={{0,16},{16,0},{2,18},{18,2},{4,20},{20,4},{6,22},{22,6},{8,24},{24... | collective-permute-start | bytes 1769480 | tf_op jit(solution)/shard_map/ppermute | solution.py:286
  84.9 2.1 %collective-permute-start.8 = (f32[1152,128]{1,0:T(8,128)S(1)}, f32[1152,128]{1,0:T(8,128)S(1)}, u32[]{:S(2)}, u32[]{:S(2)}) collective-permute-start(f32[1152,128]{1,0:T(8,128)S(1)} %shard_map.104.mine_ref), channel_id=1, source_target_pairs={{0,16},{16,0},{2,18},{18,2},{4,20},{20,4},{6,22},{22,6},{8,24},{24... | collective-permute-start | bytes 1769480 | tf_op jit(solution)/shard_map/ppermute | solution.py:291

commit v3 on v2

--- a/solution.py
+++ b/solution.py
@@ -30,13 +30,41 @@
 
 
 CORE_PAIRS = pairs_of(lambda x, y, z, c: (x, y, z, 1 - c))
-Z_TABLES = ((1, 0, 3, 2, 5, 4, 7, 6), (7, 2, 1, 4, 3, 6, 5, 0), (3, 6, 5, 0, 7, 2, 1, 4))
-Z_PAIRS = [pairs_of(lambda x, y, z, c, t=t: (x, y, t[z], c)) for t in Z_TABLES]
+Z_PAIRS = [
+    pairs_of(lambda x, y, z, c, fn=fn: (x, y, fn(z) % 8, c))
+    for fn in (
+        lambda z: z ^ 1,
+        lambda z: z + 1 if z % 2 else z - 1,
+        lambda z: z + 2 if z % 2 else z - 2,
+        lambda z: z - 3 if z % 2 == 0 else z + 3,
+    )
+]
+
+
+def turn(x, y, z, c, along_x, k):
+    return ((x + k) % 4, y, z, c) if along_x else (x, (y + k) % 4, z, c)
+
+
+FIRST_PAIRS = [pairs_of(lambda x, y, z, c, k=k: turn(x, y, z, c, c == 0, k)) for k in (1, 3, 2)]
+SECOND_PAIRS = [pairs_of(lambda x, y, z, c, k=k: turn(x, y, z, c, c == 1, k)) for k in (1, 3, 2)]
+TURNS = (1, 3, 2)
 PLANES = [
-    [flat_index(x, y, z, c) for y in range(4) for x in range(4)] for z in range(8) for c in range(2)
+    [flat_index(*((i // 4, i % 4) if c == 0 else (i % 4, i // 4)), z, c) for i in range(16)]
+    for z in range(8)
+    for c in range(2)
 ]
 VMEM = pl.BlockSpec(memory_space=pltpu.VMEM)
 SMEM = pl.BlockSpec(memory_space=pltpu.SMEM)
+
+
+HBM = pl.BlockSpec(memory_space=pltpu.HBM)
+
+
+def place():
+    row, col = lax.axis_index("row"), lax.axis_index("col")
+    core, x, y, z = row & 1, (row >> 1) & 3, (col & 1) * 2 + (row >> 3), col >> 1
+    first = jnp.where(core == 0, x, y)
+    return core, first, x + y - first, z
 
 
 def shape(dims, dtype):
@@ -51,7 +79,7 @@
         out_specs=jax.tree.map(lambda _: VMEM, outs),
         scratch_shapes=list(scratch),
         input_output_aliases=aliases or {},
-        compiler_params=pltpu.CompilerParams(vmem_limit_bytes=40 * 1024 * 1024),
+        compiler_params=pltpu.CompilerParams(vmem_limit_bytes=20 * 1024 * 1024),
         cost_estimate=pl.CostEstimate(
             flops=int(micros * 8e6), bytes_accessed=1024, transcendentals=0
         ),
@@ -62,12 +90,17 @@
     return lax.dot_general(left, right, (over, ((), ())), preferred_element_type=F32)
 
 
-def edges_body(image_ref, cot_ref, first_ref, last_ref):
-    for at, ref in enumerate((image_ref, cot_ref)):
-        head = ref[:, 0:16, :].astype(F32)
-        tail = ref[:, 16:32, :].astype(F32)
-        first_ref[at, 8:72, :] = head[:, 0, :]
-        last_ref[at, 8:72, :] = tail[:, 15, :]
+def edges_body(image_ref, cot_ref, image_out, cot_out, top_ref, low_ref, first_ref, last_ref, sem):
+    pairs = ((image_ref, image_out), (cot_ref, cot_out))
+    copies = [pltpu.make_async_copy(src, dst, sem.at[at]) for at, (src, dst) in enumerate(pairs)]
+    for copy in copies:
+        copy.start()
+    for at, ref in enumerate((image_out, cot_out)):
+        copies[at].wait()
+        top_ref[at] = ref[0]
+        low_ref[at] = ref[ROWS - 1]
+        first_ref[at, 8:72, :] = ref[:, 0:16, :].astype(F32)[:, 0, :]
+        last_ref[at, 8:72, :] = ref[:, COLS - 16 : COLS, :].astype(F32)[:, 15, :]
 
 
 def corners_body(first_ref, last_ref, above_ref, below_ref, send_first_ref, send_last_ref):
@@ -147,8 +180,9 @@
         pre_grad_ref[start : start + size, :] = grad.astype(BF16)
 
 
-def grads_body(flip, core_ref, hidden_ref, pre_grad_ref, x3_ref, c3_ref, out_ref):
-    which = core_ref[0] if flip == 0 else 1 - core_ref[0]
+def grads_body(flip, hidden_ref, pre_grad_ref, x3_ref, c3_ref, out_ref):
+    core = place()[0]
+    which = core if flip == 0 else 1 - core
 
     @pl.when(which == 0)
     def _():
@@ -169,21 +203,42 @@
                 out_ref[tap * CH : (tap + 1) * CH, :] = part[:, b * CH : (b + 1) * CH]
 
 
-def add_body(left_ref, right_ref, out_ref):
+def deal(value_of, at, size, outs):
+    for turn_by, out_ref in zip((0,) + TURNS, outs):
+        start = pl.multiple_of(((at + turn_by) & 3) * size, 8)
+        out_ref[...] = value_of(pl.ds(start, size))
+
+
+def add_body(left_ref, right_ref, *outs):
+    deal(lambda rows: left_ref[rows, :] + right_ref[rows, :], place()[1], LINES // 4, outs)
+
+
+def fold_body(own_ref, a_ref, b_ref, c_ref, *outs):
+    def value_of(rows):
+        return (own_ref[rows, :] + a_ref[rows, :]) + (b_ref[rows, :] + c_ref[rows, :])
+
+    deal(value_of, place()[2], LINES // 16, outs)
+
+
+def last_fold_body(own_ref, a_ref, b_ref, c_ref, out_ref):
+    out_ref[...] = (own_ref[...] + a_ref[...]) + (b_ref[...] + c_ref[...])
+
+
+def last_pair_body(left_ref, right_ref, out_ref):
     out_ref[...] = left_ref[...] + right_ref[...]
 
 
-def fold_body(parts_ref, out_ref):
-    total = parts_ref[0]
-    for i in range(1, 16):
-        total = total + parts_ref[i]
-    out_ref[...] = total
-
-
-def momentum_body(core_ref, grads_ref, momentum_ref, out_ref, scale_ref):
+def finish_body(own_ref, near_ref, far_ref, across_ref, out_ref):
+    total = (own_ref[...] + across_ref[...]) + (near_ref[...] + far_ref[...])
+    for i in range(16):
+        out_ref[i] = total
+
+
+def momentum_body(grads_ref, momentum_ref, out_ref, scale_ref):
+    core = place()[0]
     total = jnp.zeros((8, CH), F32)
-    for i in range(16):
-        part = grads_ref[i]
+    for start in range(0, LINES, 72):
+        part = grads_ref[start : start + 72, :]
         total = total + jnp.sum((part * part).reshape(9, 8, CH), axis=0)
     squares = jnp.sum(total)
     scale = 1.0 / jnp.sqrt(jnp.full((8, CH), squares, F32) / float(LINES * CH) + 1e-06)
@@ -191,42 +246,79 @@
     line = jnp.broadcast_to(scale[0:1], (72, CH))
     for layer in range(2):
 
-        @pl.when(core_ref[0] == layer)
+        @pl.when(core == layer)
         def _():
-            for i in range(16):
-                old = momentum_ref[pl.ds(2 * 72 * i + layer, 72, stride=2), :]
-                out_ref[i * 72 : (i + 1) * 72, :] = 0.9 * old + 0.1 * (grads_ref[i] * line)
-
-
-def mlp_body(core_ref, w_ref, b_ref, v_ref, c_ref, grads_ref, new_ref, scale_ref, k_ref, out_ref):
-    block = 48
-    gain = math.sqrt(9.0 * CH)
+            for start in range(0, LINES, 72):
+                old = momentum_ref[pl.ds(2 * start + layer, 72, stride=2), :]
+                out_ref[start : start + 72, :] = 0.9 * old + 0.1 * (grads_ref[start : start + 72, :] * line)
+
+
+PIECES = 9
+DEPTH = 80
+OUTS = 8 * (HID + 2)
+
+
+def table_body(spread_ref, out_ref):
+    row = lax.broadcasted_iota(jnp.int32, (OUTS, CH), 0) % 8
+    lane = lax.broadcasted_iota(jnp.int32, (OUTS, CH), 1)
+    same = row == lane % 8
+    total = jnp.zeros((OUTS, CH), F32)
+    for term in range(4):
+        value = jnp.broadcast_to(spread_ref[:, term : term + 1], (OUTS, CH))
+        high = value.astype(BF16).astype(F32)
+        low = value - high
+        if term == 3:
+            total = jnp.where(lane == 64, high, jnp.where(lane == 65, low, total))
+        else:
+            slots = ((high, 3 * term), (high, 3 * term + 1), (low, 3 * term + 2)) if term < 2 else ((high, 6), (low, 7))
+            for part, piece in slots:
+                total = jnp.where(same & (lane // 8 == piece), part, total)
+    out_ref[...] = total.astype(BF16)
+
+
+def mlp_body(v_ref, table_ref, grads_ref, new_ref, scale_ref, k_ref, out_ref):
+    block, blocks = 64, 6
     scale = jnp.broadcast_to(scale_ref[0:1], (block, CH))
-    base = core_ref[0] * LINES
+    base = place()[0] * LINES
+    table = table_ref[:, 0:DEPTH]
+
+    def wide(value):
+        return jnp.concatenate([value[8 * j : 8 * j + 8] for j in range(block // 8)], axis=1)
+
+    def one(start):
+        rows = pl.ds(pl.multiple_of(start, block), block)
+        parts = []
+        for value in (grads_ref[rows, :] * scale, new_ref[rows, :]):
+            high = value.astype(BF16).astype(F32)
+            parts += [wide(high), wide(value - high), wide(high)]
+        scaled = wide(k_ref[pl.ds(pl.multiple_of(base + start, block), block), :].astype(F32))
+        ones = jnp.ones_like(scaled)
+        inputs = jnp.concatenate(parts + [scaled, scaled, ones, ones], axis=0).astype(BF16)
+        halves = dot(table, inputs, ((1,), (0,)))
+        top = halves[8 * HID : 8 * HID + 8]
+        low = halves[8 * HID + 8 : 8 * HID + 16]
+        for h in range(HID):
+            half = halves[8 * h : 8 * h + 8]
+            curved = half * jnp.tanh(half)
+            top = top + v_ref[0, h] * curved
+            low = low + v_ref[1, h] * curved
+        value = top * jnp.exp(jnp.tanh(low))
+        for j in range(block // 8):
+            out_ref[pl.ds(pl.multiple_of(start + 8 * j, 8), 8), :] = value[:, j * CH : (j + 1) * CH]
 
     def step(i, _):
-        rows = pl.ds(pl.multiple_of(i * block, block), block)
-        g_hat = grads_ref[rows, :] * scale
-        new = new_ref[rows, :]
-        scaled = k_ref[pl.ds(pl.multiple_of(base + i * block, 16), block), :].astype(F32) * gain
-        top = jnp.full((block, CH), c_ref[0], F32)
-        low = jnp.full((block, CH), c_ref[1], F32)
-        for h in range(HID):
-            half = (0.5 * w_ref[h, 0]) * g_hat + (0.5 * w_ref[h, 1]) * new
-            half = half + (0.5 * w_ref[h, 2]) * scaled + 0.5 * b_ref[h]
-            unit = half + half * jnp.tanh(half)
-            top = top + v_ref[0, h] * unit
-            low = low + v_ref[1, h] * unit
-        out_ref[rows, :] = top * jnp.exp(jnp.tanh(low))
+        for j in range(blocks):
+            one((i * blocks + j) * block)
         return 0
 
-    lax.fori_loop(0, LINES // block, step, 0)
-
-
-def weave_body(core_ref, mine_ref, theirs_ref, out_ref):
+    lax.fori_loop(0, LINES // (block * blocks), step, 0)
+
+
+def weave_body(mine_ref, theirs_ref, out_ref):
+    core = place()[0]
     for layer in range(2):
 
-        @pl.when(core_ref[0] == layer)
+        @pl.when(core == layer)
         def _():
             for start in range(0, LINES, 72):
                 out_ref[pl.ds(2 * start + layer, 72, stride=2), :] = mine_ref[start : start + 72, :]
@@ -236,15 +328,21 @@
 def on_device(
     features, cotangent, kernels, momentum, mlp_in_weight, mlp_in_bias, mlp_out_weight, mlp_out_bias
 ):
-    core = (lax.axis_index("row") % 2).astype(jnp.int32).reshape(1)
     count_r, count_c = lax.axis_size("row"), lax.axis_size("col")
     up = lambda n: [(i, (i + 1) % n) for i in range(n)]
     down = lambda n: [((i + 1) % n, i) for i in range(n)]
 
-    above = lax.ppermute(jnp.stack([features[-1], cotangent[-1]]), "row", up(count_r))
-    below = lax.ppermute(jnp.stack([features[0], cotangent[0]]), "row", down(count_r))
-    columns = (shape((2, EDGE, CH), F32),) * 2
-    first, last = call(edges_body, [VMEM] * 2, columns, 0.5)(features, cotangent)
+    line, column = shape((2, COLS, CH), BF16), shape((2, EDGE, CH), F32)
+    whole = shape((ROWS, COLS, CH), BF16)
+    features, cotangent, top, low, first, last = call(
+        edges_body,
+        [HBM] * 2,
+        (whole, whole, line, line, column, column),
+        1.5,
+        [pltpu.SemaphoreType.DMA((2,))],
+    )(features, cotangent)
+    above = lax.ppermute(low, "row", up(count_r))
+    below = lax.ppermute(top, "row", down(count_r))
     columns = (shape((2, EDGE, CH), BF16),) * 2
     first, last = call(corners_body, [VMEM] * 4, columns, 0.2)(first, last, above, below)
     left = lax.ppermute(last, "col", up(count_c))
@@ -264,34 +362,38 @@
     )(x3, c3, pre, back, left, right, kernels)
 
     layer = shape((LINES, CH), F32)
-    gradient = lambda flip: call(functools.partial(grads_body, flip), [SMEM] + [VMEM] * 4, layer, 2.5)(
-        core, hidden, pre_grad, x3, c3
+    gradient = lambda flip: call(functools.partial(grads_body, flip), [VMEM] * 4, layer, 1.5)(
+        hidden, pre_grad, x3, c3
     )
     theirs = lax.ppermute(gradient(1), AXES, CORE_PAIRS)
-    mine = call(add_body, [VMEM] * 2, layer, 0.3)(gradient(0), theirs)
-    parts = lax.all_to_all(
-        mine.reshape(16, LINES // 16, CH), AXES, 0, 0, axis_index_groups=PLANES, tiled=True
-    )
-    part = call(fold_body, [VMEM], shape((LINES // 16, CH), F32), 0.3)(parts)
-    for pairs in Z_PAIRS:
-        part = part + lax.ppermute(part, AXES, pairs)
-    grads = lax.all_to_all(
-        jnp.broadcast_to(part[None], parts.shape), AXES, 0, 0, axis_index_groups=PLANES, tiled=True
-    )
+    quarter, part = shape((LINES // 4, CH), F32), shape((LINES // 16, CH), F32)
+    own, *sent = call(add_body, [VMEM] * 2, (quarter,) * 4, 0.3)(gradient(0), theirs)
+    got = [lax.ppermute(s, AXES, pairs) for s, pairs in zip(sent, FIRST_PAIRS)]
+    own, *sent = call(fold_body, [VMEM] * 4, (part,) * 4, 0.3)(own, *got)
+    got = [lax.ppermute(s, AXES, pairs) for s, pairs in zip(sent, SECOND_PAIRS)]
+    own = call(last_fold_body, [VMEM] * 4, part, 0.2)(own, *got)
+    own = call(last_pair_body, [VMEM] * 2, part, 0.2)(own, lax.ppermute(own, AXES, Z_PAIRS[0]))
+    got = [lax.ppermute(own, AXES, pairs) for pairs in Z_PAIRS[1:]]
+    copies = call(finish_body, [VMEM] * 4, shape((16, LINES // 16, CH), F32), 0.2)(own, *got)
+    grads = lax.all_to_all(copies, AXES, 0, 0, axis_index_groups=PLANES, tiled=True)
+    grads = grads.reshape(LINES, CH)
 
     woven = momentum.reshape(2, LINES, CH).transpose(1, 0, 2).reshape(2 * LINES, CH)
-    new, scale = call(momentum_body, [SMEM, VMEM, VMEM], (layer, shape((8, CH), F32)), 0.5)(
-        core, grads, woven
-    )
+    new, scale = call(momentum_body, [VMEM] * 2, (layer, shape((8, CH), F32)), 0.5)(grads, woven)
     new_theirs = lax.ppermute(new, AXES, CORE_PAIRS)
-    update = call(mlp_body, [SMEM] * 5 + [VMEM] * 4, layer, 8.0)(
-        core, mlp_in_weight, mlp_in_bias, mlp_out_weight, mlp_out_bias,
-        grads.reshape(LINES, CH), new, scale, kernels.reshape(2 * LINES, CH),
-    )
+    gain = jnp.array([1.0, 1.0, math.sqrt(9.0 * CH), 1.0], F32)
+    terms = 0.5 * jnp.concatenate([mlp_in_weight, mlp_in_bias[:, None]], axis=1) * gain
+    linear = jnp.sum(mlp_out_weight[:, :, None] * terms[None], axis=1)
+    linear = linear + jnp.pad(mlp_out_bias[:, None], ((0, 0), (3, 0)))
+    spread = jnp.repeat(jnp.concatenate([terms, linear]), 8, axis=0)
+    table = call(table_body, [VMEM], shape((OUTS, CH), BF16), 0.5)(spread)
+    update = call(
+        mlp_body, [SMEM] + [VMEM] * 5, layer, 5.0
+    )(mlp_out_weight, table, grads, new, scale, kernels.reshape(2 * LINES, CH))
     update_theirs = lax.ppermute(update, AXES, CORE_PAIRS)
     outs = []
-    for own, other in ((update, update_theirs), (new, new_theirs)):
-        both = call(weave_body, [SMEM] + [VMEM] * 2, shape((2 * LINES, CH), F32), 0.5)(core, own, other)
+    for mine, other in ((update, update_theirs), (new, new_theirs)):
+        both = call(weave_body, [VMEM] * 2, shape((2 * LINES, CH), F32), 0.5)(mine, other)
         outs.append(both.reshape(LINES, 2, CH).transpose(1, 0, 2).reshape(2, LINES * CH))
     return tuple(outs)
 

time: 88.5 us -> 85 us (0.960)
  blocking collectives: 14.3 us -> 0 us
  waiting for transfers between devices: 16.7 us -> 27.8 us
  starting transfers between devices: 33 us -> 37.3 us
  Pallas kernels: 18.5 us -> 16 us
  local copies, waits for them, and re-layouts: 4.91 us -> 2.48 us
    all_to_all x1 -> x0, blocking collectives: 14.3 us -> none  [on_device(): lax.all_to_all(mine.reshape(16, LINES // 16, CH), AXES, 0, 0, axis_index_...]
    ppermute x5 -> x12, waiting for transfers between devices: 5.99 us -> 17.7 us  [the longest x3 5.49 us: on_device(): got = [lax.ppermute(s, AXES, pairs) for s, pairs in zip(sent, FIRST_PAIRS)]]
    ppermute x5 -> x12, starting transfers between devices: 9.42 us -> 15.3 us  [the longest x3 4.76 us: on_device(): got = [lax.ppermute(own, AXES, pairs) for pairs in Z_PAIRS[1:]]]
    ppermute x1, starting transfers between devices: 5.06 us -> 1.03 us  [on_device(): theirs = lax.ppermute(gradient(1), AXES, CORE_PAIRS)]
    pallas_call x9 -> x13, Pallas kernels: 14.8 us -> 12.3 us  [the longest x1 6.29 us: on_device(): call(mlp_body, [SMEM] + [VMEM] * 5, layer, 5.0)]
    ppermute x1, starting transfers between devices: 6.59 us -> 7.76 us  [on_device(): new_theirs = lax.ppermute(new, AXES, CORE_PAIRS)]
    unnamed x21 -> x18, local copies, waits for them, and re-layouts: 3.24 us -> 2.18 us
  transfers between devices with their start and end apart: 11 -> 18, of which waited for: 6 -> 13; matrix products, arithmetic and copies ran while one was open for 0% -> 1% of each run, Pallas kernels for 17% -> 13%
where the time goes in v3:
time: 85 us; the launch traced here: 84.7 us
  starting transfers between devices  37.3 us (44%)
  waiting for transfers between devices  27.8 us (33%)
  Pallas kernels  16 us (19%)
  local copies, waits for them, and re-layouts  2.48 us (3%)
  between operations  0.85 us (1%)
    all_to_all x1, waiting for transfers between devices, on_device(): lax.all_to_all(copies, AXES, 0, 0, axis_index_groups=PLANES, tiled=True)  8.72 us
    ppermute x1, starting transfers between devices, on_device(): new_theirs = lax.ppermute(new, AXES, CORE_PAIRS)  7.76 us
    pallas_call x1, Pallas kernels, on_device(): call(mlp_body, [SMEM] + [VMEM] * 5, layer, 5.0)  6.29 us
    ppermute x3, waiting for transfers between devices, on_device(): got = [lax.ppermute(s, AXES, pairs) for s, pairs in zip(sent, FIRST_PAIRS)]  5.49 us
    ppermute x1, starting transfers between devices, on_device(): right = lax.ppermute(first, 'col', down(count_c))  5.38 us
    ppermute x3, starting transfers between devices, on_device(): got = [lax.ppermute(own, AXES, pairs) for pairs in Z_PAIRS[1:]]  4.76 us
    all_to_all x1, starting transfers between devices, on_device(): lax.all_to_all(copies, AXES, 0, 0, axis_index_groups=PLANES, tiled=True)  4.39 us
    ppermute x3, starting transfers between devices, on_device(): got = [lax.ppermute(s, AXES, pairs) for s, pairs in zip(sent, SECOND_PAIRS)]  4.35 us
  transfers between devices with their start and end apart: 18, of which 13 were waited for; matrix products, arithmetic and copies ran while one was open for 1% of the time, Pallas kernels for 13%

profile of v3, /device:TPU:1, one launch (start us, length us, event | category | flops | bytes accessed | tf_op | source)
XLA Modules:
  0.0 84.7 jit_solution(6156729735830155431)
XLA Ops:
  0.6 0.0 copy-start
  0.6 1.1 %copy-done.2 = bf16[64,32,128]{2,1,0:T(8,128)(2,1)S(1)} copy-done((bf16[64,32,128]{2,1,0:T(8,128)(2,1)S(1)}, bf16[64,32,128]{2,1,0:T(8,128)(2,1)}, u32[]{:S(2)}) %copy-start.2) | copy-done | bytes 524312
  1.7 1.0 %copy-done.3 = bf16[64,32,128]{2,1,0:T(8,128)(2,1)S(1)} copy-done((bf16[64,32,128]{2,1,0:T(8,128)(2,1)S(1)}, bf16[64,32,128]{2,1,0:T(8,128)(2,1)}, u32[]{:S(2)}) %copy-start.3) | copy-done | bytes 524312
  2.8 0.2 shard_map.105
  3.0 2.7 %collective-permute-start = (bf16[2,32,128]{2,1,0:T(8,128)(2,1)S(1)}, bf16[2,32,128]{2,1,0:T(8,128)(2,1)S(1)}, u32[]{:S(2)}, u32[]{:S(2)}) collective-permute-start(bf16[2,32,128]{2,1,0:T(8,128)(2,1)S(1)} %get-tuple-element.30), channel_id=1, source_target_pairs={{0,16},{16,32},{32,48},{48,64},{64,80},{80,96},{96,112},{112,128},... | collective-permute-start | bytes 49160 | tf_op jit(solution)/shard_map/ppermute | solution.py:344
  5.7 0.7 collective-permute-start.1
  6.4 0.6 collective-permute-done.above_ref
  6.9 1.9 %collective-permute-done.1.below_ref = bf16[2,32,128]{2,1,0:T(8,128)(2,1)S(1)} collective-permute-done((bf16[2,32,128]{2,1,0:T(8,128)(2,1)S(1)}, bf16[2,32,128]{2,1,0:T(8,128)(2,1)S(1)}, u32[]{:S(2)}, u32[]{:S(2)}) %collective-permute-start.1) | collective-permute-done | bytes 16416 | tf_op jit(solution)/shard_map/ppermute | solution.py:345
  8.8 3.3 %collective-permute-start.2 = (bf16[2,80,128]{2,1,0:T(8,128)(2,1)S(1)}, bf16[2,80,128]{2,1,0:T(8,128)(2,1)S(1)}, u32[]{:S(2)}, u32[]{:S(2)}) collective-permute-start(bf16[2,80,128]{2,1,0:T(8,128)(2,1)S(1)} %get-tuple-element.38), channel_id=1, source_target_pairs={{0,1},{1,2},{2,3},{3,4},{4,5},{5,6},{6,7},{7,8},{8,9},{9,10},{10,1... | collective-permute-start | bytes 122888 | tf_op jit(solution)/shard_map/ppermute | solution.py:348
  12.1 5.4 %collective-permute-start.3 = (bf16[2,80,128]{2,1,0:T(8,128)(2,1)S(1)}, bf16[2,80,128]{2,1,0:T(8,128)(2,1)S(1)}, u32[]{:S(2)}, u32[]{:S(2)}) collective-permute-start(bf16[2,80,128]{2,1,0:T(8,128)(2,1)S(1)} %get-tuple-element.39), channel_id=1, source_target_pairs={{1,0},{2,1},{3,2},{4,3},{5,4},{6,5},{7,6},{8,7},{9,8},{10,9},{11,1... | collective-permute-start | bytes 122888 | tf_op jit(solution)/shard_map/ppermute | solution.py:349
  17.5 2.7 %shard_map.106 = (bf16[2112,384]{1,0:T(8,128)(2,1)S(1)}, bf16[2112,384]{1,0:T(8,128)(2,1)S(1)}, f32[2048,128]{1,0:T(8,128)S(1)}, f32[2048,128]{1,0:T(8,128)S(1)}) custom-call(bf16[64,32,128]{2,1,0:T(8,128)(2,1)S(1)} %get-tuple-element.28.image_ref, bf16[64,32,128]{2,1,0:T(8,128)(2,1)S(1)} %get-tuple-element.29.cot_ref, ...), custom_call_target="tpu_custom_call" | custom-call | flops 40000000 | bytes 1024 | tf_op jit(solution)/shard_map/pallas_call | solution.py:351
  20.2 0.0 collective-permute-done.2.left_ref
  20.2 0.0 collective-permute-done.3.right_ref
  20.2 0.9 %shard_map.108 = (bf16[2112,384]{1,0:T(8,128)(2,1)S(1)}, bf16[2112,384]{1,0:T(8,128)(2,1)S(1)}, bf16[2048,128]{1,0:T(8,128)(2,1)S(1)}, bf16[2048,128]{1,0:T(8,128)(2,1)S(1)}) custom-call(bf16[2112,384]{1,0:T(8,128)(2,1)S(1)} %get-tuple-element.32.x3_ref, ...), custom_call_target="tpu_custom_call", output_to_operand_aliasing={{0}: (0, {}), {1}: (1, {})} | custom-call | flops 12000000 | bytes 1024 | tf_op jit(solution)/shard_map/pallas_call | solution.py:355
  21.2 1.1 %shard_map.110 = f32[1152,128]{1,0:T(8,128)S(1)} custom-call(bf16[2048,128]{1,0:T(8,128)(2,1)S(1)} %get-tuple-element.40.hidden_ref, bf16[2048,128]{1,0:T(8,128)(2,1)S(1)} %get-tuple-element.41.pre_grad_ref, bf16[2112,384]{1,0:T(8,128)(2,1)S(1)} %get-tuple-element.42.x3_ref, bf16[2112,384]{1,0:T(8,128)(2,1)S(1)} %get-tuple-element.43.c3_ref), custom_call_target="tpu_custom_call" | custom-call | flops 12000000 | bytes 1024 | tf_op jit(solution)/shard_map/pallas_call | solution.py:365
  22.3 1.0 %collective-permute-start.4 = (f32[1152,128]{1,0:T(8,128)S(1)}, f32[1152,128]{1,0:T(8,128)S(1)}, u32[]{:S(2)}, u32[]{:S(2)}) collective-permute-start(f32[1152,128]{1,0:T(8,128)S(1)} %shard_map.110), channel_id=1, source_target_pairs={{0,16},{16,0},{2,18},{18,2},{4,20},{20,4},{6,22},{22,6},{8,24},{24... | collective-permute-start | bytes 1769480 | tf_op jit(solution)/shard_map/ppermute | solution.py:368
  23.3 1.0 %shard_map.109.left_ref = f32[1152,128]{1,0:T(8,128)S(1)} custom-call(bf16[2048,128]{1,0:T(8,128)(2,1)S(1)} %get-tuple-element.40.hidden_ref, bf16[2048,128]{1,0:T(8,128)(2,1)S(1)} %get-tuple-element.41.pre_grad_ref, bf16[2112,384]{1,0:T(8,128)(2,1)S(1)} %get-tuple-element.42.x3_ref, bf16[2112,384]{1,0:T(8,128)(2,1)S(1)} %get-tuple-element.43.c3_ref), custom_call_target="tpu_custom_call" | custom-call | flops 12000000 | bytes 1024 | tf_op jit(solution)/shard_map/pallas_call | solution.py:365
  24.4 0.0 copy-start.5
  24.4 0.0 copy-start.6
  24.4 0.0 copy-start.7
  24.4 0.0 copy-start.4
  24.4 0.0 copy-start.8
  24.4 0.5 collective-permute-done.4.right_ref
  25.0 0.1 shard_map.111
  25.0 0.0 copy-start.1
  25.0 0.5 collective-permute-start.5
  25.5 2.3 %collective-permute-start.6 = (f32[288,128]{1,0:T(8,128)S(1)}, f32[288,128]{1,0:T(8,128)S(1)}, u32[]{:S(2)}, u32[]{:S(2)}) collective-permute-start(f32[288,128]{1,0:T(8,128)S(1)} %get-tuple-element.46), channel_id=1, source_target_pairs={{0,96},{16,145},{2,98},{18,147},{4,100},{20,149},{6,102},{22,151},... | collective-permute-start | bytes 442376 | tf_op jit(solution)/shard_map/ppermute | solution.py:371
  27.8 0.0 collective-permute-start.7
  27.8 2.8 %collective-permute-done.5.a_ref = f32[288,128]{1,0:T(8,128)S(1)} collective-permute-done((f32[288,128]{1,0:T(8,128)S(1)}, f32[288,128]{1,0:T(8,128)S(1)}, u32[]{:S(2)}, u32[]{:S(2)}) %collective-permute-start.5) | collective-permute-done | bytes 147488 | tf_op jit(solution)/shard_map/ppermute | solution.py:371
  30.6 0.8 collective-permute-done.6.b_ref
  31.5 1.8 %collective-permute-done.7.c_ref = f32[288,128]{1,0:T(8,128)S(1)} collective-permute-done((f32[288,128]{1,0:T(8,128)S(1)}, f32[288,128]{1,0:T(8,128)S(1)}, u32[]{:S(2)}, u32[]{:S(2)}) %collective-permute-start.7) | collective-permute-done | bytes 147488 | tf_op jit(solution)/shard_map/ppermute | solution.py:371
  33.3 1.7 %collective-permute-start.10 = (f32[72,128]{1,0:T(8,128)S(1)}, f32[72,128]{1,0:T(8,128)S(1)}, u32[]{:S(2)}, u32[]{:S(2)}) collective-permute-start(f32[72,128]{1,0:T(8,128)S(1)} %get-tuple-element.51), channel_id=1, source_target_pairs={{0,1},{16,80},{2,3},{18,82},{4,5},{20,84},{6,7},{22,86},{8,9},{24,... | collective-permute-start | bytes 110600 | tf_op jit(solution)/shard_map/ppermute | solution.py:373
  35.0 2.7 %collective-permute-start.8 = (f32[72,128]{1,0:T(8,128)S(1)}, f32[72,128]{1,0:T(8,128)S(1)}, u32[]{:S(2)}, u32[]{:S(2)}) collective-permute-start(f32[72,128]{1,0:T(8,128)S(1)} %get-tuple-element.49), channel_id=1, source_target_pairs={{0,128},{16,48},{2,130},{18,50},{4,132},{20,52},{6,134},{22,54},{8... | collective-permute-start | bytes 110600 | tf_op jit(solution)/shard_map/ppermute | solution.py:373
  37.7 0.0 collective-permute-start.9
  37.7 0.0 collective-permute-done.10.c_ref
  37.7 1.3 %collective-permute-done.8.a_ref = f32[72,128]{1,0:T(8,128)S(1)} collective-permute-done((f32[72,128]{1,0:T(8,128)S(1)}, f32[72,128]{1,0:T(8,128)S(1)}, u32[]{:S(2)}, u32[]{:S(2)}) %collective-permute-start.8) | collective-permute-done | bytes 36896 | tf_op jit(solution)/shard_map/ppermute | solution.py:373
  39.0 1.7 %collective-permute-done.9.b_ref = f32[72,128]{1,0:T(8,128)S(1)} collective-permute-done((f32[72,128]{1,0:T(8,128)S(1)}, f32[72,128]{1,0:T(8,128)S(1)}, u32[]{:S(2)}, u32[]{:S(2)}) %collective-permute-start.9) | collective-permute-done | bytes 36896 | tf_op jit(solution)/shard_map/ppermute | solution.py:373
  40.8 0.1 collective-permute-start.11
  40.9 0.1 maximum_multiply_fusion
  41.0 2.7 %collective-permute-done.11.right_ref = f32[72,128]{1,0:T(8,128)S(1)} collective-permute-done((f32[72,128]{1,0:T(8,128)S(1)}, f32[72,128]{1,0:T(8,128)S(1)}, u32[]{:S(2)}, u32[]{:S(2)}) %collective-permute-start.11) | collective-permute-done | bytes 36896 | tf_op jit(solution)/shard_map/ppermute | solution.py:375
  43.7 1.9 %collective-permute-start.12 = (f32[72,128]{1,0:T(8,128)S(1)}, f32[72,128]{1,0:T(8,128)S(1)}, u32[]{:S(2)}, u32[]{:S(2)}) collective-permute-start(f32[72,128]{1,0:T(8,128)S(1)} %shard_map.114.own_ref), channel_id=1, source_target_pairs={{0,14},{16,30},{2,4},{18,20},{4,2},{20,18},{6,8},{22,24},{8,6},{24... | collective-permute-start | bytes 110600 | tf_op jit(solution)/shard_map/ppermute | solution.py:376
  45.5 1.2 %collective-permute-start.13 = (f32[72,128]{1,0:T(8,128)S(1)}, f32[72,128]{1,0:T(8,128)S(1)}, u32[]{:S(2)}, u32[]{:S(2)}) collective-permute-start(f32[72,128]{1,0:T(8,128)S(1)} %shard_map.114.own_ref), channel_id=1, source_target_pairs={{0,12},{16,28},{2,6},{18,22},{4,0},{20,16},{6,10},{22,26},{8,4},{2... | collective-permute-start | bytes 110600 | tf_op jit(solution)/shard_map/ppermute | solution.py:376
  46.8 1.7 %collective-permute-start.14 = (f32[72,128]{1,0:T(8,128)S(1)}, f32[72,128]{1,0:T(8,128)S(1)}, u32[]{:S(2)}, u32[]{:S(2)}) collective-permute-start(f32[72,128]{1,0:T(8,128)S(1)} %shard_map.114.own_ref), channel_id=1, source_target_pairs={{0,10},{16,26},{2,8},{18,24},{4,14},{20,30},{6,12},{22,28},{8,2},{... | collective-permute-start | bytes 110600 | tf_op jit(solution)/shard_map/ppermute | solution.py:376
  48.4 0.1 multiply_reduce_fusion
  48.5 0.1 copy.18
  48.6 0.0 collective-permute-done.12.near_ref
  48.6 0.6 collective-permute-done.13.far_ref
  49.3 3.4 %collective-permute-done.14.across_ref = f32[72,128]{1,0:T(8,128)S(1)} collective-permute-done((f32[72,128]{1,0:T(8,128)S(1)}, f32[72,128]{1,0:T(8,128)S(1)}, u32[]{:S(2)}, u32[]{:S(2)}) %collective-permute-start.14) | collective-permute-done | bytes 36896 | tf_op jit(solution)/shard_map/ppermute | solution.py:376
  52.6 0.9 %shard_map.115 = f32[16,72,128]{2,1,0:T(8,128)} custom-call(f32[72,128]{1,0:T(8,128)S(1)} %shard_map.114.own_ref, f32[72,128]{1,0:T(8,128)S(1)} %collective-permute-done.12.near_ref, f32[72,128]{1,0:T(8,128)S(1)} %collective-permute-done.13.far_ref, f32[72,128]{1,0:T(8,128)S(1)} %collective-permute-done.14.across_ref), custom_call_target="tpu_custom_call" | custom-call | flops 1600000 | bytes 1024 | tf_op jit(solution)/shard_map/pallas_call | solution.py:377
  53.5 4.4 %all-to-all-start = ((f32[16,72,128]{2,1,0:T(8,128)}), f32[16,72,128]{2,1,0:T(8,128)S(1)}, u32[]{:S(2)}, u32[]{:S(2)}) async-start(f32[16,72,128]{2,1,0:T(8,128)} %shard_map.115), calls=%async_computation | async-start | bytes 1179648 | tf_op jit(solution)/shard_map/all_to_all | solution.py:378
  57.9 0.1 pad_add_fusion
  57.9 0.1 copy.19
  58.0 0.1 pad_maximum_fusion
  58.1 0.1 copy.20
  58.2 0.2 shard_map.104.table_ref
  58.5 8.7 %all-to-all-done = f32[16,72,128]{2,1,0:T(8,128)S(1)} async-done(((f32[16,72,128]{2,1,0:T(8,128)}), f32[16,72,128]{2,1,0:T(8,128)S(1)}, u32[]{:S(2)}, u32[]{:S(2)}) %all-to-all-start) | async-done | bytes 589856 | tf_op jit(solution)/shard_map/all_to_all | solution.py:378
  67.2 0.3 shard_map.116
  67.5 7.8 %collective-permute-start.16 = (f32[1152,128]{1,0:T(8,128)S(1)}, f32[1152,128]{1,0:T(8,128)S(1)}, u32[]{:S(2)}, u32[]{:S(2)}) collective-permute-start(f32[1152,128]{1,0:T(8,128)S(1)} %get-tuple-element.52.new_ref.mine_ref), channel_id=1, source_target_pairs={{0,16},{16,0},{2,18},{18,2},{4,20},{20,4},{6,22},{22,6},{8,24},{24... | collective-permute-start | bytes 1769480 | tf_op jit(solution)/shard_map/ppermute | solution.py:383
  75.3 6.3 %shard_map.117.mine_ref = f32[1152,128]{1,0:T(8,128)S(1)} custom-call(f32[2,32]{1,0:T(2,128)S(1)} %copy-done.4, bf16[272,128]{1,0:T(8,128)(2,1)S(1)} %shard_map.104.table_ref, f32[1152,128]{1,0:T(8,128)S(1)} %bitcast.23, f32[1152,128]{1,0:T(8,128)S(1)} %get-tuple-element.52.new_ref.mine_ref, f32[8,128]{1,0:T(8,128)S(1)} %get-tuple-element.53.scale_ref, ...), custom_call_target="tpu_custom_call" | custom-call | flops 40000000 | bytes 1024 | tf_op jit(solution)/shard_map/pallas_call | solution.py:390
  81.5 0.1 collective-permute-start.15
  81.7 0.0 collective-permute-done.16.theirs_ref
  81.7 1.1 %shard_map.119 = f32[2304,128]{1,0:T(8,128)} custom-call(f32[1152,128]{1,0:T(8,128)S(1)} %get-tuple-element.52.new_ref.mine_ref, f32[1152,128]{1,0:T(8,128)S(1)} %collective-permute-done.16.theirs_ref), custom_call_target="tpu_custom_call" | custom-call | flops 4000000 | bytes 1024 | tf_op jit(solution)/shard_map/pallas_call | solution.py:396
  82.8 0.9 %collective-permute-done.15.theirs_ref = f32[1152,128]{1,0:T(8,128)S(1)} collective-permute-done((f32[1152,128]{1,0:T(8,128)S(1)}, f32[1152,128]{1,0:T(8,128)S(1)}, u32[]{:S(2)}, u32[]{:S(2)}) %collective-permute-start.15) | collective-permute-done | bytes 589856 | tf_op jit(solution)/shard_map/ppermute | solution.py:393
  83.6 1.1 %shard_map.118 = f32[2304,128]{1,0:T(8,128)} custom-call(f32[1152,128]{1,0:T(8,128)S(1)} %shard_map.117.mine_ref, f32[1152,128]{1,0:T(8,128)S(1)} %collective-permute-done.15.theirs_ref), custom_call_target="tpu_custom_call" | custom-call | flops 4000000 | bytes 1024 | tf_op jit(solution)/shard_map/pallas_call | solution.py:396
  (14 shorter events, 0.1 us)
Async XLA Ops:
  0.6 16.9 %copy-start = (bf16[2,9,128,128]{3,2,1,0:T(8,128)(2,1)S(1)}, bf16[2,9,128,128]{3,2,1,0:T(8,128)(2,1)}, u32[]{:S(2)}) copy-start(bf16[2,9,128,128]{3,2,1,0:T(8,128)(2,1)} %k_ref.3) | copy-start | bytes 1769476
  0.6 1.1 %copy-start.2 = (bf16[64,32,128]{2,1,0:T(8,128)(2,1)S(1)}, bf16[64,32,128]{2,1,0:T(8,128)(2,1)}, u32[]{:S(2)}) copy-start(bf16[64,32,128]{2,1,0:T(8,128)(2,1)} %image_ref.1) | copy-start | bytes 1572868
  1.7 1.0 %copy-start.3 = (bf16[64,32,128]{2,1,0:T(8,128)(2,1)S(1)}, bf16[64,32,128]{2,1,0:T(8,128)(2,1)}, u32[]{:S(2)}) copy-start(bf16[64,32,128]{2,1,0:T(8,128)(2,1)} %cot_ref.1) | copy-start | bytes 1572868
  3.0 4.0 %collective-permute-start = (bf16[2,32,128]{2,1,0:T(8,128)(2,1)S(1)}, bf16[2,32,128]{2,1,0:T(8,128)(2,1)S(1)}, u32[]{:S(2)}, u32[]{:S(2)}) collective-permute-start(bf16[2,32,128]{2,1,0:T(8,128)(2,1)S(1)} %get-tuple-element.30), channel_id=1, source_target_pairs={{0,16},{16,32},{32,48},{48,64},{64,80},{80,96},{96,112},{112,128},... | collective-permute-start | bytes 49160 | tf_op jit(solution)/shard_map/ppermute | solution.py:344
  5.7 3.2 %collective-permute-start.1 = (bf16[2,32,128]{2,1,0:T(8,128)(2,1)S(1)}, bf16[2,32,128]{2,1,0:T(8,128)(2,1)S(1)}, u32[]{:S(2)}, u32[]{:S(2)}) collective-permute-start(bf16[2,32,128]{2,1,0:T(8,128)(2,1)S(1)} %get-tuple-element.31), channel_id=1, source_target_pairs={{16,0},{32,16},{48,32},{64,48},{80,64},{96,80},{112,96},{128,112},... | collective-permute-start | bytes 49160 | tf_op jit(solution)/shard_map/ppermute | solution.py:345
  8.8 11.4 %collective-permute-start.2 = (bf16[2,80,128]{2,1,0:T(8,128)(2,1)S(1)}, bf16[2,80,128]{2,1,0:T(8,128)(2,1)S(1)}, u32[]{:S(2)}, u32[]{:S(2)}) collective-permute-start(bf16[2,80,128]{2,1,0:T(8,128)(2,1)S(1)} %get-tuple-element.38), channel_id=1, source_target_pairs={{0,1},{1,2},{2,3},{3,4},{4,5},{5,6},{6,7},{7,8},{8,9},{9,10},{10,1... | collective-permute-start | bytes 122888 | tf_op jit(solution)/shard_map/ppermute | solution.py:348
  12.1 8.1 %collective-permute-start.3 = (bf16[2,80,128]{2,1,0:T(8,128)(2,1)S(1)}, bf16[2,80,128]{2,1,0:T(8,128)(2,1)S(1)}, u32[]{:S(2)}, u32[]{:S(2)}) collective-permute-start(bf16[2,80,128]{2,1,0:T(8,128)(2,1)S(1)} %get-tuple-element.39), channel_id=1, source_target_pairs={{1,0},{2,1},{3,2},{4,3},{5,4},{6,5},{7,6},{8,7},{9,8},{10,9},{11,1... | collective-permute-start | bytes 122888 | tf_op jit(solution)/shard_map/ppermute | solution.py:349
  22.3 2.7 %collective-permute-start.4 = (f32[1152,128]{1,0:T(8,128)S(1)}, f32[1152,128]{1,0:T(8,128)S(1)}, u32[]{:S(2)}, u32[]{:S(2)}) collective-permute-start(f32[1152,128]{1,0:T(8,128)S(1)} %shard_map.110), channel_id=1, source_target_pairs={{0,16},{16,0},{2,18},{18,2},{4,20},{20,4},{6,22},{22,6},{8,24},{24... | collective-permute-start | bytes 1769480 | tf_op jit(solution)/shard_map/ppermute | solution.py:368
  24.4 16.5 %copy-start.5 = (f32[32,3]{0,1:T(4,128)S(1)}, f32[32,3]{0,1:T(4,128)}, u32[]{:S(2)}) copy-start(f32[32,3]{0,1:T(4,128)} %param.13) | copy-start | bytes 1156
  24.4 16.5 %copy-start.6 = (f32[32]{0:T(128)S(1)}, f32[32]{0:T(128)}, u32[]{:S(2)}) copy-start(f32[32]{0:T(128)} %param.14) | copy-start | bytes 388
  24.4 16.5 %copy-start.7 = (f32[4]{0:T(128)S(1)}, f32[4]{0:T(128)}, u32[]{:S(2)}) copy-start(f32[4]{0:T(128)} %constant.11) | copy-start | bytes 52
  24.4 24.0 %copy-start.4 = (f32[2,32]{1,0:T(2,128)S(1)}, f32[2,32]{1,0:T(2,128)}, u32[]{:S(2)}) copy-start(f32[2,32]{1,0:T(2,128)} %v_ref.1) | copy-start | bytes 772
  24.4 24.1 %copy-start.8 = (f32[2]{0:T(128)S(1)}, f32[2]{0:T(128)}, u32[]{:S(2)}) copy-start(f32[2]{0:T(128)} %param.16) | copy-start | bytes 28
  25.0 42.2 %copy-start.1 = (f32[2,147456]{1,0:T(2,128)S(1)}, f32[2,147456]{1,0:T(2,128)}, u32[]{:S(2)}) copy-start(f32[2,147456]{1,0:T(2,128)} %param.12) | copy-start | bytes 3538948
  25.0 5.6 %collective-permute-start.5 = (f32[288,128]{1,0:T(8,128)S(1)}, f32[288,128]{1,0:T(8,128)S(1)}, u32[]{:S(2)}, u32[]{:S(2)}) collective-permute-start(f32[288,128]{1,0:T(8,128)S(1)} %get-tuple-element.45), channel_id=1, source_target_pairs={{0,32},{16,144},{2,34},{18,146},{4,36},{20,148},{6,38},{22,150},{8... | collective-permute-start | bytes 442376 | tf_op jit(solution)/shard_map/ppermute | solution.py:371
  25.5 5.9 %collective-permute-start.6 = (f32[288,128]{1,0:T(8,128)S(1)}, f32[288,128]{1,0:T(8,128)S(1)}, u32[]{:S(2)}, u32[]{:S(2)}) collective-permute-start(f32[288,128]{1,0:T(8,128)S(1)} %get-tuple-element.46), channel_id=1, source_target_pairs={{0,96},{16,145},{2,98},{18,147},{4,100},{20,149},{6,102},{22,151},... | collective-permute-start | bytes 442376 | tf_op jit(solution)/shard_map/ppermute | solution.py:371
  27.8 5.5 %collective-permute-start.7 = (f32[288,128]{1,0:T(8,128)S(1)}, f32[288,128]{1,0:T(8,128)S(1)}, u32[]{:S(2)}, u32[]{:S(2)}) collective-permute-start(f32[288,128]{1,0:T(8,128)S(1)} %get-tuple-element.47), channel_id=1, source_target_pairs={{0,64},{16,17},{2,66},{18,19},{4,68},{20,21},{6,70},{22,23},{8,72}... | collective-permute-start | bytes 442376 | tf_op jit(solution)/shard_map/ppermute | solution.py:371
  33.3 4.4 %collective-permute-start.10 = (f32[72,128]{1,0:T(8,128)S(1)}, f32[72,128]{1,0:T(8,128)S(1)}, u32[]{:S(2)}, u32[]{:S(2)}) collective-permute-start(f32[72,128]{1,0:T(8,128)S(1)} %get-tuple-element.51), channel_id=1, source_target_pairs={{0,1},{16,80},{2,3},{18,82},{4,5},{20,84},{6,7},{22,86},{8,9},{24,... | collective-permute-start | bytes 110600 | tf_op jit(solution)/shard_map/ppermute | solution.py:373
  35.0 4.0 %collective-permute-start.8 = (f32[72,128]{1,0:T(8,128)S(1)}, f32[72,128]{1,0:T(8,128)S(1)}, u32[]{:S(2)}, u32[]{:S(2)}) collective-permute-start(f32[72,128]{1,0:T(8,128)S(1)} %get-tuple-element.49), channel_id=1, source_target_pairs={{0,128},{16,48},{2,130},{18,50},{4,132},{20,52},{6,134},{22,54},{8... | collective-permute-start | bytes 110600 | tf_op jit(solution)/shard_map/ppermute | solution.py:373
  37.7 3.1 %collective-permute-start.9 = (f32[72,128]{1,0:T(8,128)S(1)}, f32[72,128]{1,0:T(8,128)S(1)}, u32[]{:S(2)}, u32[]{:S(2)}) collective-permute-start(f32[72,128]{1,0:T(8,128)S(1)} %get-tuple-element.50), channel_id=1, source_target_pairs={{0,129},{16,112},{2,131},{18,114},{4,133},{20,116},{6,135},{22,118... | collective-permute-start | bytes 110600 | tf_op jit(solution)/shard_map/ppermute | solution.py:373
  40.8 2.9 %collective-permute-start.11 = (f32[72,128]{1,0:T(8,128)S(1)}, f32[72,128]{1,0:T(8,128)S(1)}, u32[]{:S(2)}, u32[]{:S(2)}) collective-permute-start(f32[72,128]{1,0:T(8,128)S(1)} %shard_map.113.left_ref), channel_id=1, source_target_pairs={{0,2},{16,18},{2,0},{18,16},{4,6},{20,22},{6,4},{22,20},{8,10},{24... | collective-permute-start | bytes 110600 | tf_op jit(solution)/shard_map/ppermute | solution.py:375
  43.7 4.9 %collective-permute-start.12 = (f32[72,128]{1,0:T(8,128)S(1)}, f32[72,128]{1,0:T(8,128)S(1)}, u32[]{:S(2)}, u32[]{:S(2)}) collective-permute-start(f32[72,128]{1,0:T(8,128)S(1)} %shard_map.114.own_ref), channel_id=1, source_target_pairs={{0,14},{16,30},{2,4},{18,20},{4,2},{20,18},{6,8},{22,24},{8,6},{24... | collective-permute-start | bytes 110600 | tf_op jit(solution)/shard_map/ppermute | solution.py:376
  45.5 3.7 %collective-permute-start.13 = (f32[72,128]{1,0:T(8,128)S(1)}, f32[72,128]{1,0:T(8,128)S(1)}, u32[]{:S(2)}, u32[]{:S(2)}) collective-permute-start(f32[72,128]{1,0:T(8,128)S(1)} %shard_map.114.own_ref), channel_id=1, source_target_pairs={{0,12},{16,28},{2,6},{18,22},{4,0},{20,16},{6,10},{22,26},{8,4},{2... | collective-permute-start | bytes 110600 | tf_op jit(solution)/shard_map/ppermute | solution.py:376
  46.8 5.8 %collective-permute-start.14 = (f32[72,128]{1,0:T(8,128)S(1)}, f32[72,128]{1,0:T(8,128)S(1)}, u32[]{:S(2)}, u32[]{:S(2)}) collective-permute-start(f32[72,128]{1,0:T(8,128)S(1)} %shard_map.114.own_ref), channel_id=1, source_target_pairs={{0,10},{16,26},{2,8},{18,24},{4,14},{20,30},{6,12},{22,28},{8,2},{... | collective-permute-start | bytes 110600 | tf_op jit(solution)/shard_map/ppermute | solution.py:376
  53.5 13.7 %all-to-all-start = ((f32[16,72,128]{2,1,0:T(8,128)}), f32[16,72,128]{2,1,0:T(8,128)S(1)}, u32[]{:S(2)}, u32[]{:S(2)}) async-start(f32[16,72,128]{2,1,0:T(8,128)} %shard_map.115), calls=%async_computation | async-start | bytes 1179648 | tf_op jit(solution)/shard_map/all_to_all | solution.py:378
  67.5 14.2 %collective-permute-start.16 = (f32[1152,128]{1,0:T(8,128)S(1)}, f32[1152,128]{1,0:T(8,128)S(1)}, u32[]{:S(2)}, u32[]{:S(2)}) collective-permute-start(f32[1152,128]{1,0:T(8,128)S(1)} %get-tuple-element.52.new_ref.mine_ref), channel_id=1, source_target_pairs={{0,16},{16,0},{2,18},{18,2},{4,20},{20,4},{6,22},{22,6},{8,24},{24... | collective-permute-start | bytes 1769480 | tf_op jit(solution)/shard_map/ppermute | solution.py:383
  81.5 2.1 %collective-permute-start.15 = (f32[1152,128]{1,0:T(8,128)S(1)}, f32[1152,128]{1,0:T(8,128)S(1)}, u32[]{:S(2)}, u32[]{:S(2)}) collective-permute-start(f32[1152,128]{1,0:T(8,128)S(1)} %shard_map.117.mine_ref), channel_id=1, source_target_pairs={{0,16},{16,0},{2,18},{18,2},{4,20},{20,4},{6,22},{22,6},{8,24},{24... | collective-permute-start | bytes 1769480 | tf_op jit(solution)/shard_map/ppermute | solution.py:393
